TPU v7x, 32 devices: a whole 2x2x4 slice. The times are simulated.
32 devices in a mesh: rows: 8 (over y, x, core), rhs: 4 (over z).
Axes of the slice: x: 2, y: 2, z: 4, core: 2. Of those that a mesh axis runs over, the one named last changes fastest.
Arguments:
- sources: bfloat16 [32768, 2048], P('rows', 'rhs'), may hold values from -6 to 6
- near_blocks: bfloat16 [128, 3, 256, 256], P('rows'), may hold values from -0.21875 to 0.21875
- near_list: int32 [128, 3], P('rows'), may hold values from 0 to 127, as said below
- source_basis: bfloat16 [128, 256, 32], P('rows'), may hold values from -0.375 to 0.375
- target_basis: bfloat16 [128, 256, 32], P('rows'), may hold values from -0.375 to 0.375
- transfer_fine: bfloat16 [224, 32, 32], P('rows'), may hold values from -0.875 to 0.875
- transfer_coarse: bfloat16 [32, 32, 32], P('rhs'), may hold values from -0.875 to 0.875
- couple_fine: bfloat16 [224, 3, 32, 32], P('rows'), may hold values from -0.625 to 0.625
- couple_coarse: bfloat16 [32, 3, 32, 32], P('rhs'), may hold values from -0.625 to 0.625
- far_fine: int32 [224, 3], P('rows'), may hold values from 0 to 127, as said below
- far_coarse: int32 [32, 3], replicated, may hold values from -1 to 15, as said below
Outputs:
- potentials: bfloat16 [32768, 2048], P('rows', 'rhs')
Inputs may be any that keep to these rules, and one draw needn't show every extreme that they name: `near_list`: row t lists the leaf clusters t - 1, t and t + 1 modulo 128 in some order. `far_fine`: row d * 28 + o + i belongs to cluster d * m + i of the level with n = m * 8 clusters, where (o, m) is (0, 16), (16, 8) or (24, 4). It lists, in some order, the three clusters of that level that are children of the cyclic neighbours of the cluster's parent and not cyclic neighbours of the cluster: for cluster j with parent p = j // 2, the clusters 2p - 2, 2p + 2, 2p + 3 if j is even and 2p - 2, 2p - 1, 2p + 3 if j is odd, modulo n. `far_coarse`: row n + j for n = 8, 16, ..., 16 lists, in some order, the three far clusters of cluster j of the level with n clusters by the rule of far_fine. Row 4 + j holds (j + 2) modulo 4 in slot 0 and -1 in slots 1 and 2. Rows 0 to 3 hold -1.
All inputs are finite; a program needn't handle non-finite values.
Results may differ from a plain program's by a relative error of at most 0.012.
Values may be sent and summed in bfloat16 or wider, within the bound.
A program may use at most 128 MiB of HBM per device.

v0:
```python
import jax
import jax.numpy as jnp
from jax import lax
from jax.experimental import pallas as pl
from jax.experimental.pallas import tpu as pltpu
from jax.sharding import PartitionSpec as P

MESH = pl.DeviceIdType.MESH
F32 = jnp.float32
BF16 = jnp.bfloat16


def dot(a, b):
    return lax.dot_general(a, b, (((1,), (0,)), ((), ())), preferred_element_type=F32)


def dot_t(a, b):
    return lax.dot_general(a, b, (((0,), (0,)), ((), ())), preferred_element_type=F32)


def kernel(
    dims,
    x_hbm,
    near_hbm,
    near_list,
    sb_hbm,
    ef_hbm,
    ec_hbm,
    sf_hbm,
    sc_hbm,
    far_fine,
    far_coarse,
    part_hbm,
    f_hbm,
    xw,
    near,
    sb,
    ef,
    ec,
    sf,
    sc,
    wf,
    wc,
    cw0,
    cw1,
    cw2,
    cw3,
    cr,
    cu,
    fr,
    f3,
    f2,
    f1,
    f0,
    part,
    load_sem,
    out_sem,
    halo_send,
    halo_recv,
    table_send,
    table_recv,
    gather_send,
    gather_recv,
    pair_send,
    pair_recv,
):
    count, leaf, rank, R, T, chunks = dims
    me = lax.axis_index("rows")
    z = lax.axis_index("rhs")
    right, left = lax.rem(me + 1, R), lax.rem(me + R - 1, R)
    per = count // chunks
    block = ec.shape[0]

    loads = [
        pltpu.make_async_copy(ec_hbm, ec, load_sem.at[0]),
        pltpu.make_async_copy(sc_hbm, sc, load_sem.at[1]),
        pltpu.make_async_copy(sb_hbm, sb, load_sem.at[2]),
    ]
    x_loads = [
        pltpu.make_async_copy(
            x_hbm.at[pl.ds(c * per, per)], xw.at[pl.ds(1 + c * per, per)], load_sem.at[7 + c]
        )
        for c in range(chunks)
    ]
    late = [
        pltpu.make_async_copy(ef_hbm, ef, load_sem.at[3]),
        pltpu.make_async_copy(sf_hbm, sf, load_sem.at[4]),
        pltpu.make_async_copy(near_hbm, near, load_sem.at[5]),
    ]
    for copy in loads + x_loads + late[:2]:
        copy.start()

    barrier = pltpu.get_barrier_semaphore()
    for k in range(1, R):
        pl.semaphore_signal(
            barrier, inc=1, device_id=(lax.rem(me + k, R), z), device_id_type=MESH
        )
    for k in range(1, T):
        pl.semaphore_signal(
            barrier, inc=1, device_id=(me, lax.rem(z + k, T)), device_id_type=MESH
        )

    loads[0].wait()
    loads[1].wait()
    for r in range(block):
        wc[z * block + r] = jnp.concatenate([sc[r, 0], sc[r, 1], sc[r, 2], ec[r]], axis=1)
    pl.semaphore_wait(barrier, R + T - 2)

    def send(src, dst, send_sem, recv_sem, row, col):
        return pltpu.make_async_remote_copy(
            src_ref=src,
            dst_ref=dst,
            send_sem=send_sem,
            recv_sem=recv_sem,
            device_id=(row, col),
            device_id_type=MESH,
        )

    low = send(
        x_hbm.at[pl.ds(0, 1)],
        xw.at[pl.ds(count + 1, 1)],
        halo_send.at[8],
        halo_recv.at[8],
        left,
        z,
    )
    high = send(
        x_hbm.at[pl.ds(count - 1, 1)],
        xw.at[pl.ds(0, 1)],
        halo_send.at[9],
        halo_recv.at[9],
        right,
        z,
    )
    low.start()
    high.start()
    edges = [low, high]

    pair_rows = wc.at[pl.ds(2 * R + 2 * me, 2)]
    pair_owner = (2 * R + 2 * me) // block
    coarse_blocks = (2 * R + block - 1) // block
    mine = wc.at[pl.ds(z * block, block)]

    def pair_copy(k, source, target):
        return send(pair_rows, pair_rows, pair_send.at[k], pair_recv.at[source], me, target)

    def table_copy(k, source, target):
        return send(mine, mine, table_send.at[k], table_recv.at[source], me, target)

    @pl.when(z == pair_owner)
    def _():
        for k in range(1, T):
            pair_copy(k, z, lax.rem(z + k, T)).start()

    @pl.when(z < coarse_blocks)
    def _():
        for k in range(1, T):
            table_copy(k, z, lax.rem(z + k, T)).start()

    def halo(ref, width, size, level):
        low = send(
            ref.at[pl.ds(width, width)],
            ref.at[pl.ds(width + size, width)],
            halo_send.at[2 * level],
            halo_recv.at[2 * level],
            left,
            z,
        )
        high = send(
            ref.at[pl.ds(size, width)],
            ref.at[pl.ds(0, width)],
            halo_send.at[2 * level + 1],
            halo_recv.at[2 * level + 1],
            right,
            z,
        )
        low.start()
        high.start()
        return [low, high]

    loads[2].wait()
    for c in range(chunks):
        x_loads[c].wait()
    late[2].start()
    for c in range(chunks):
        for t in range(c * per, (c + 1) * per):
            cw0[2 + t] = dot(sb[t], xw[1 + t]).astype(BF16)
    windows = [cw0, cw1, cw2, cw3]
    sizes = [count, count // 2, count // 4, count // 8]
    firsts = [0, count, count + count // 2]
    late[0].wait()
    for level in range(3):
        below, above = windows[level], windows[level + 1]
        for j in range(sizes[level + 1]):
            pair = below[2 + 2 * j : 4 + 2 * j].reshape(2 * rank, -1)
            first = firsts[level] + 2 * j
            matrix = ef[first : first + 2].reshape(2 * rank, rank)
            above[2 + j] = dot_t(matrix, pair).astype(BF16)

    @pl.when(z != pair_owner)
    def _():
        pair_copy(0, pair_owner, lax.rem(z + 1, T)).wait_recv()

    def transfer(row):
        return wc[row][:, 3 * rank :]

    own = dot_t(transfer(2 * R + 2 * me), cw3[2]) + dot_t(transfer(2 * R + 2 * me + 1), cw3[3])
    cr[me] = own.astype(BF16)
    gathers = []
    for k in range(1, R):
        spot = cr.at[pl.ds(me, 1)]
        copy = send(
            spot, spot, gather_send.at[k], gather_recv.at[me], lax.rem(me + k, R), z
        )
        copy.start()
        gathers.append(copy)
    halos = [None] * 4
    for level in (3, 2, 1, 0):
        halos[level] = halo(windows[level], 2, sizes[level], level)

    late[1].wait()
    for j in range(wf.shape[0]):
        wf[j] = jnp.concatenate([sf[j, 0], sf[j, 1], sf[j, 2], ef[j]], axis=1)

    total = count * R
    late[2].wait()

    def near_leaf(t):
        total_sum = None
        for wanted in (-1, 0, 1):
            target = lax.rem(me * count + t + wanted + total, total)
            slot = jnp.where(
                near_list[0, t] == target, 0, jnp.where(near_list[1, t] == target, 1, 2)
            )
            term = dot(near[t, slot], xw[1 + t + wanted])
            total_sum = term if total_sum is None else total_sum + term
        return total_sum

    def near_step(i, carry):
        for u in range(2):
            t = 1 + 2 * i + u
            part[t] = near_leaf(t).astype(BF16)
        return carry

    lax.fori_loop(0, (count - 2) // 2, near_step, 0)
    stores = [
        pltpu.make_async_copy(
            part.at[pl.ds(1, count - 2)], part_hbm.at[pl.ds(1, count - 2)], out_sem.at[0]
        ),
        pltpu.make_async_copy(part.at[pl.ds(0, 1)], part_hbm.at[pl.ds(0, 1)], out_sem.at[1]),
        pltpu.make_async_copy(
            part.at[pl.ds(count - 1, 1)], part_hbm.at[pl.ds(count - 1, 1)], out_sem.at[2]
        ),
    ]
    stores[0].start()
    edges[0].wait_recv()
    part[count - 1] = near_leaf(count - 1).astype(BF16)
    edges[1].wait_recv()
    part[0] = near_leaf(0).astype(BF16)
    stores[1].start()
    stores[2].start()

    for k in range(1, R):
        other = lax.rem(me + k, R)
        spot = cr.at[pl.ds(other, 1)]
        send(spot, spot, gather_send.at[k], gather_recv.at[other], other, z).wait_recv()

    for k in range(1, T):
        other = lax.rem(z + k, T)
        theirs = wc.at[pl.ds(other * block, block)]

        @pl.when(other < coarse_blocks)
        def _():
            send(theirs, theirs, table_send.at[0], table_recv.at[other], me, other).wait_recv()

    def coarse(n, index):
        return cr[index] if n == R else cu[n - 4 + index]

    n = R // 2
    while n >= 4:
        for j in range(n):
            lifted = dot_t(transfer(2 * n + 2 * j), coarse(2 * n, 2 * j)) + dot_t(
                transfer(2 * n + 2 * j + 1), coarse(2 * n, 2 * j + 1)
            )
            cu[n - 4 + j] = lifted.astype(BF16)
        n //= 2
    n = 4
    value = None
    while n <= R:
        row = n + me // (R // n)
        if n == 4:
            value = dot(wc[row][:, :rank], coarse(n, far_coarse[0, row]))
        else:
            parts = [coarse(n, far_coarse[s, row]) for s in range(3)] + [value]
            value = dot(wc[row], jnp.concatenate(parts, axis=0))
        value = value.astype(BF16)
        n *= 2
    fr[0] = value

    def wait_halo(level):
        for copy in halos[level]:
            copy.wait_recv()

    wait_halo(3)
    for i in range(2):
        row = 2 * R + 2 * me + i
        parts = [
            cw3[jnp.minimum(lax.rem(far_coarse[s, row] - 2 * me + 2 + 2 * R, 2 * R), 5)]
            for s in range(3)
        ] + [fr[0]]
        f3[i] = dot(wc[row], jnp.concatenate(parts, axis=0)).astype(BF16)
    above = f3
    for level, below in ((2, f2), (1, f1), (0, f0)):
        wait_halo(level)
        m = sizes[level]
        n = m * R
        for i in range(m):
            row = firsts[level] + i
            parts = [
                windows[level][jnp.minimum(lax.rem(far_fine[s, row] - m * me + 2 + n, n), m + 3)]
                for s in range(3)
            ] + [above[i // 2]]
            below[i] = dot(wf[row], jnp.concatenate(parts, axis=0)).astype(BF16)
        above = below

    last = pltpu.make_async_copy(f0, f_hbm, out_sem.at[3])
    last.start()

    @pl.when(z == pair_owner)
    def _():
        for k in range(1, T):
            pair_copy(k, z, lax.rem(z + k, T)).wait_send()

    @pl.when(z < coarse_blocks)
    def _():
        for k in range(1, T):
            table_copy(k, z, lax.rem(z + k, T)).wait_send()

    for copy in gathers + edges:
        copy.wait_send()
    for pair in halos:
        for copy in pair:
            copy.wait_send()
    for copy in stores:
        copy.wait()
    last.wait()


def finish(part, tb, f, out):
    for t in range(part.shape[0]):
        out[t] = (part[t].astype(F32) + dot_t(tb[t], f[t])).astype(BF16)


def body(
    sources,
    near_blocks,
    near_list,
    source_basis,
    target_basis,
    transfer_fine,
    transfer_coarse,
    couple_fine,
    couple_coarse,
    far_fine,
    far_coarse,
):
    count, _, leaf, _ = near_blocks.shape
    rank = source_basis.shape[2]
    width = sources.shape[1]
    R, T = lax.axis_size("rows"), lax.axis_size("rhs")
    fine = transfer_fine.shape[0]
    block = transfer_coarse.shape[0]
    chunks = 4
    dims = (count, leaf, rank, R, T, chunks)
    anyspace = pl.BlockSpec(memory_space=pl.ANY)
    smem = pl.BlockSpec(memory_space=pltpu.SMEM)

    def moments(clusters):
        return pltpu.VMEM((clusters, rank, width), BF16)

    part, far = pl.pallas_call(
        lambda *refs: kernel(dims, *refs),
        name="tree_apply",
        out_shape=[
            jax.ShapeDtypeStruct((count, leaf, width), BF16),
            jax.ShapeDtypeStruct((count, rank, width), BF16),
        ],
        in_specs=[anyspace] * 2 + [smem] + [anyspace] * 5 + [smem] * 2,
        out_specs=[anyspace, anyspace],
        scratch_shapes=[
            pltpu.VMEM((count + 2, leaf, width), BF16),
            pltpu.VMEM(near_blocks.shape, BF16),
            pltpu.VMEM((count, rank, leaf), BF16),
            pltpu.VMEM(transfer_fine.shape, BF16),
            pltpu.VMEM(transfer_coarse.shape, BF16),
            pltpu.VMEM(couple_fine.shape, BF16),
            pltpu.VMEM(couple_coarse.shape, BF16),
            pltpu.VMEM((fine, rank, 4 * rank), BF16),
            pltpu.VMEM((block * T, rank, 4 * rank), BF16),
            moments(count + 4),
            moments(count // 2 + 4),
            moments(count // 4 + 4),
            moments(count // 8 + 4),
            moments(R),
            moments(R),
            moments(1),
            moments(count // 8),
            moments(count // 4),
            moments(count // 2),
            moments(count),
            pltpu.VMEM((count, leaf, width), BF16),
            pltpu.SemaphoreType.DMA((7 + chunks,)),
            pltpu.SemaphoreType.DMA((4,)),
            pltpu.SemaphoreType.DMA((10,)),
            pltpu.SemaphoreType.DMA((10,)),
            pltpu.SemaphoreType.DMA((T,)),
            pltpu.SemaphoreType.DMA((T,)),
            pltpu.SemaphoreType.DMA((R,)),
            pltpu.SemaphoreType.DMA((R,)),
            pltpu.SemaphoreType.DMA((T,)),
            pltpu.SemaphoreType.DMA((T,)),
        ],
        compiler_params=pltpu.CompilerParams(
            collective_id=0, has_side_effects=True, vmem_limit_bytes=63 * 1024 * 1024
        ),
    )(
        sources.reshape(count, leaf, width),
        near_blocks,
        near_list.T,
        jnp.swapaxes(source_basis, 1, 2),
        transfer_fine,
        transfer_coarse,
        couple_fine,
        couple_coarse,
        far_fine.T,
        far_coarse.T,
    )
    step = 4
    block_of = lambda *tail: pl.BlockSpec((step,) + tail, lambda i: (i, 0, 0))
    out = pl.pallas_call(
        finish,
        name="far_add",
        grid=(count // step,),
        out_shape=jax.ShapeDtypeStruct((count, leaf, width), BF16),
        in_specs=[block_of(leaf, width), block_of(rank, leaf), block_of(rank, width)],
        out_specs=block_of(leaf, width),
        compiler_params=pltpu.CompilerParams(vmem_limit_bytes=63 * 1024 * 1024),
    )(part, jnp.swapaxes(target_basis, 1, 2), far)
    return out.reshape(count * leaf, width)


def solution(mesh):
    in_specs = (
        P("rows", "rhs"),
        P("rows", None, None, None),
        P("rows", None),
        P("rows", None, None),
        P("rows", None, None),
        P("rows", None, None),
        P("rhs", None, None),
        P("rows", None, None, None),
        P("rhs", None, None, None),
        P("rows", None),
        P(),
    )
    out_specs = P("rows", "rhs")
    return jax.shard_map(body, mesh=mesh, in_specs=in_specs, out_specs=out_specs, check_vma=False)
```

profile of v0, /device:TPU:0, one launch (start us, length us, event | category | flops | bytes accessed | tf_op | source)
XLA Modules:
  0.0 29.4 jit_solution(8771028041910363492)
XLA Ops:
  0.0 23.7 %tree_apply.1 = (bf16[16,256,512]{2,1,0:T(8,128)(2,1)}, bf16[16,32,512]{2,1,0:T(8,128)(2,1)}) custom-call(bf16[16,256,512]{2,1,0:T(8,128)(2,1)} %bitcast.7, bf16[16,3,256,256]{3,2,1,0:T(8,128)(2,1)} %refs_1_.1, s32[3,16]{1,0:T(4,128)} %bitcast.10, bf16[16,32,256]{2,1,0:T(8,128)(2,1)} %bitcast.8, bf16[28,32,32]{2,1,0:T(8,128)(2,1)} %refs_4_.1, ...), custom_call_target="tpu_custom_call" | custom-call | tf_op jit(solution)/shard_map/tree_apply/pallas_call | solution.py:381
  23.7 5.7 %far_add.1 = bf16[16,256,512]{2,1,0:T(8,128)(2,1)} custom-call(bf16[16,256,512]{2,1,0:T(8,128)(2,1)} %get-tuple-element.7.part, bf16[16,32,256]{2,1,0:T(8,128)(2,1)} %bitcast.9, bf16[16,32,512]{2,1,0:T(8,128)(2,1)} %get-tuple-element.8.f), custom_call_target="tpu_custom_call" | custom-call | tf_op jit(solution)/shard_map/far_add/pallas_call | solution.py:440
where the time goes:
time: 29.6 us; the launch traced here: 29.4 us
  Pallas kernels  29.4 us (99%)
    pallas_call x1, Pallas kernels, body(): pl.pallas_call(lambda *refs: kernel(dims, *refs), name='tree_apply', out_...  23.7 us
    pallas_call x1, Pallas kernels, body(): pl.pallas_call(finish, name='far_add', grid=(count // step,), out_shape=j...  5.69 us

commit v1 on v0

v1 whole, which is shorter than its diff:
```python
import jax
import jax.numpy as jnp
from jax import lax
from jax.experimental import pallas as pl
from jax.experimental.pallas import tpu as pltpu
from jax.sharding import PartitionSpec as P

MESH = pl.DeviceIdType.MESH
F32 = jnp.float32
BF16 = jnp.bfloat16
MIB = 1024 * 1024


def dot(a, b):
    return lax.dot_general(a, b, (((1,), (0,)), ((), ())), preferred_element_type=F32)


def dot_t(a, b):
    return lax.dot_general(a, b, (((0,), (0,)), ((), ())), preferred_element_type=F32)


def kernel(
    dims,
    x_hbm,
    near_hbm,
    near_list_hbm,
    sb_hbm,
    tb_hbm,
    ef_hbm,
    ec_hbm,
    sf_hbm,
    sc_hbm,
    far_fine_hbm,
    far_coarse_hbm,
    part,
    tt,
    f0,
    top,
    near_list,
    far_fine,
    far_coarse,
    xw,
    near,
    sb,
    tb,
    ef,
    ec,
    sf,
    sc,
    wf,
    wc,
    cw0,
    cw1,
    cw2,
    cw3,
    cr,
    cu,
    f3,
    f2,
    f1,
    edge_sum,
    lifts,
    q1,
    q0,
    load_sem,
    edge_send,
    edge_recv,
    halo_send,
    halo_recv,
    table_send,
    table_recv,
    gather_send,
    gather_recv,
    pair_send,
    pair_recv,
    lift_send,
    lift_recv,
    hello,
):
    count, leaf, rank, R, T, spans, pieces = dims
    me = lax.axis_index("rows")
    z = lax.axis_index("rhs")
    right, left = lax.rem(me + 1, R), lax.rem(me + R - 1, R)
    parity = lax.rem(me, 2)
    twin = me + 1 - 2 * parity
    block = ec.shape[0]
    sizes = [count, count // 2, count // 4, count // 8]
    firsts = [0, count, count + count // 2]
    windows = [cw0, cw1, cw2, cw3]

    def load(source, target, k):
        copy = pltpu.make_async_copy(source, target, load_sem.at[k])
        copy.start()
        return copy

    barrier = pltpu.get_barrier_semaphore()
    for k in range(1, R):
        pl.semaphore_signal(
            barrier, inc=1, device_id=(lax.rem(me + k, R), z), device_id_type=MESH
        )
    for k in range(1, T):

        @pl.when(z + k < T)
        def _():
            pl.semaphore_signal(barrier, inc=1, device_id=(me, z + k), device_id_type=MESH)

    edge_loads = [
        load(x_hbm.at[pl.ds(0, 1)], xw.at[pl.ds(1, 1)], 0),
        load(x_hbm.at[pl.ds(count - 1, 1)], xw.at[pl.ds(count, 1)], 1),
    ]
    load_sb = load(sb_hbm, sb, 2)
    x_loads = [
        load(x_hbm.at[pl.ds(a, b - a)], xw.at[pl.ds(1 + a, b - a)], 16 + c)
        for c, (a, b) in enumerate(spans)
    ]
    load_ef = load(ef_hbm, ef, 3)
    load_ec = load(ec_hbm, ec, 4)
    load_sc = load(sc_hbm, sc, 5)
    load_lists = [
        load(near_list_hbm, near_list, 6),
        load(far_fine_hbm, far_fine, 7),
        load(far_coarse_hbm, far_coarse, 8),
    ]

    def send(src, dst, send_sem, recv_sem, row, col):
        return pltpu.make_async_remote_copy(
            src_ref=src,
            dst_ref=dst,
            send_sem=send_sem,
            recv_sem=recv_sem,
            device_id=(row, col),
            device_id_type=MESH,
        )

    def both(low_src, low_dst, high_src, high_dst, send_sem, recv_sem, k):
        low = send(low_src, low_dst, send_sem.at[2 * k], recv_sem.at[2 * k], left, z)
        high = send(high_src, high_dst, send_sem.at[2 * k + 1], recv_sem.at[2 * k + 1], right, z)
        low.start()
        high.start()
        return [low, high]

    for copy in edge_loads:
        copy.wait()
    pl.semaphore_wait(barrier, R - 1 + z)
    for k in range(1, T):

        @pl.when(z >= k)
        def _():
            pl.semaphore_signal(hello, inc=1, device_id=(me, z - k), device_id_type=MESH)

    rows = leaf // pieces

    def edge_piece(k):
        span = pl.ds(k * rows, rows)
        return both(
            xw.at[1, span],
            xw.at[count + 1, span],
            xw.at[count, span],
            xw.at[0, span],
            edge_send,
            edge_recv,
            k,
        )

    edges = [edge_piece(k) for k in range(pieces // 2)]

    load_sb.wait()

    def leaf_moment(t):
        cw0[2 + t] = dot(sb[t], xw[1 + t]).astype(BF16)

    leaf_moment(0)
    leaf_moment(count - 1)
    for c, (a, b) in enumerate(spans):
        x_loads[c].wait()
        for t in range(a, b):
            leaf_moment(t)
    load_near = load(near_hbm, near, 9)
    load_sf = load(sf_hbm, sf, 10)
    load_tb = load(tb_hbm, tb, 11)

    load_ef.wait()

    def pair_matrix(level, j):
        first = firsts[level] + 2 * j
        return ef[first : first + 2].reshape(2 * rank, rank)

    low_pack = [pair_matrix(level, 0) for level in range(3)]
    high_pack = [pair_matrix(level, sizes[level + 1] - 1) for level in range(3)]
    lifts[0] = jnp.concatenate(low_pack + low_pack[:1], axis=1)
    lifts[1] = jnp.concatenate(high_pack + high_pack[:1], axis=1)

    halos = [None] * 4
    for level in range(3):
        below, above = windows[level], windows[level + 1]
        for j in range(sizes[level + 1]):
            pair = below[2 + 2 * j : 4 + 2 * j].reshape(2 * rank, -1)
            above[2 + j] = dot_t(pair_matrix(level, j), pair).astype(BF16)
        if level == 0:
            tables = both(
                lifts.at[0], lifts.at[3], lifts.at[1], lifts.at[2], lift_send, lift_recv, 0
            )
            halos[0] = both(
                cw0.at[pl.ds(2, 2)],
                cw0.at[pl.ds(2 + count, 2)],
                cw0.at[pl.ds(count, 2)],
                cw0.at[pl.ds(0, 2)],
                halo_send,
                halo_recv,
                0,
            )

    def inner_halo(level):
        ref, size = windows[level], sizes[level]
        return both(
            ref.at[pl.ds(3, 1)],
            ref.at[pl.ds(size + 3, 1)],
            ref.at[pl.ds(size, 1)],
            ref.at[pl.ds(0, 1)],
            halo_send,
            halo_recv,
            level,
        )

    load_ec.wait()
    load_sc.wait()
    for r in range(block):
        wc[z * block + r] = jnp.concatenate([sc[r, 0], sc[r, 1], sc[r, 2], ec[r]], axis=1)
    for level in (1, 2, 3):
        halos[level] = inner_halo(level)
    edges += [edge_piece(k) for k in range(pieces // 2, pieces)]

    pair_rows = wc.at[pl.ds(2 * R + 2 * me, 2)]
    pair_owner = (2 * R + 2 * me) // block
    coarse_blocks = (2 * R + block - 1) // block
    mine = wc.at[pl.ds(z * block, block)]

    def pair_copy(k, source, target):
        return send(pair_rows, pair_rows, pair_send.at[k], pair_recv.at[source], me, target)

    def table_copy(k, source, target):
        return send(mine, mine, table_send.at[k], table_recv.at[source], me, target)

    for copy in load_lists:
        copy.wait()
    total = count * R

    def near_term(t, wanted):
        target = lax.rem(me * count + t + wanted + total, total)
        slot = jnp.where(
            near_list[0, t] == target, 0, jnp.where(near_list[1, t] == target, 1, 2)
        )
        return dot(near[t, slot], xw[1 + t + wanted])

    def near_leaf(t):
        part[t] = (near_term(t, -1) + near_term(t, 0) + near_term(t, 1)).astype(BF16)

    def near_step(i, carry):
        for u in range(2):
            near_leaf(1 + 2 * i + u)
        return carry

    steps = (count - 2) // 2
    load_near.wait()

    @pl.when(z > 0)
    def _():
        @pl.when(z == pair_owner)
        def _():
            for k in range(1, T):

                @pl.when(z >= k)
                def _():
                    pair_copy(k, z, z - k).start()

        @pl.when(z < coarse_blocks)
        def _():
            for k in range(1, T):

                @pl.when(z >= k)
                def _():
                    table_copy(k, z, z - k).start()

    lax.fori_loop(0, steps // 2, near_step, 0)

    @pl.when(z < T - 1)
    def _():
        pl.semaphore_wait(hello, T - 1 - z)

    @pl.when(z == pair_owner)
    def _():
        for k in range(1, T):

            @pl.when(z < k)
            def _():
                pair_copy(k, z, lax.rem(z - k + T, T)).start()

    @pl.when(z < coarse_blocks)
    def _():
        for k in range(1, T):

            @pl.when(z < k)
            def _():
                table_copy(k, z, lax.rem(z - k + T, T)).start()

    lax.fori_loop(steps // 2, steps, near_step, 0)

    @pl.when(z != pair_owner)
    def _():
        pair_copy(0, pair_owner, lax.rem(z + 1, T)).wait_recv()

    def transfer(row):
        return wc[row][:, 3 * rank :]

    own = dot_t(transfer(2 * R + 2 * me), cw3[2]) + dot_t(transfer(2 * R + 2 * me + 1), cw3[3])
    cr[me] = own.astype(BF16)

    def gather_copy(source, target, k):
        spot = cr.at[pl.ds(source, 1)]
        return send(spot, spot, gather_send.at[k], gather_recv.at[source], target, z)

    gathers = []
    for k in range(1, R // 2):
        gathers.append(gather_copy(me, lax.rem(me + 2 * k, R), k))
    gathers.append(gather_copy(me, twin, 0))
    for copy in gathers:
        copy.start()

    edge_sum[0] = near_term(0, 0) + near_term(0, 1)
    edge_sum[1] = near_term(count - 1, -1) + near_term(count - 1, 0)

    load_sf.wait()
    for j in range(wf.shape[0]):
        wf[j] = jnp.concatenate([sf[j, 0], sf[j, 1], sf[j, 2], ef[j]], axis=1)

    for j in range(sizes[2]):
        both_rows = dot(pair_matrix(1, j), ef[firsts[2] + j]).astype(BF16)
        q1[2 * j : 2 * j + 2] = both_rows.reshape(2, rank, rank)
    for j in range(sizes[1]):
        both_rows = dot(pair_matrix(0, j), q1[j]).astype(BF16)
        q0[2 * j : 2 * j + 2] = both_rows.reshape(2, rank, rank)
    across = lax.broadcasted_iota(jnp.int32, (rank, rank), 0)
    down = lax.broadcasted_iota(jnp.int32, (rank, rank), 1)
    unit = jnp.where(across == down, 1.0, 0.0).astype(BF16)
    load_tb.wait()
    for t in range(count):
        tt[t] = dot_t(tb[t], jnp.concatenate([unit, q0[t]], axis=1)).astype(BF16)

    for copy in tables:
        copy.wait_recv()
    for copy in halos[0]:
        copy.wait_recv()
    for level in range(3):
        below, above = windows[level], windows[level + 1]
        size = sizes[level]
        for copy in halos[level + 1]:
            copy.wait_recv()
        from_left = lifts[2][:, level * rank : (level + 1) * rank]
        from_right = lifts[3][:, level * rank : (level + 1) * rank]
        low_pair = below[0:2].reshape(2 * rank, -1)
        high_pair = below[size + 2 : size + 4].reshape(2 * rank, -1)
        above[1] = dot_t(from_left, low_pair).astype(BF16)
        above[size // 2 + 2] = dot_t(from_right, high_pair).astype(BF16)

    for i in range(2):
        row = 2 * R + 2 * me + i
        parts = [
            cw3[jnp.minimum(lax.rem(far_coarse[s, row] - 2 * me + 2 + 2 * R, 2 * R), 5)]
            for s in range(3)
        ]
        f3[i] = dot(wc[row][:, : 3 * rank], jnp.concatenate(parts, axis=0)).astype(BF16)
    upper = f3
    for level, below in ((2, f2), (1, f1), (0, f0)):
        m = sizes[level]
        n = m * R
        for i in range(m):
            row = firsts[level] + i
            parts = [
                windows[level][jnp.minimum(lax.rem(far_fine[s, row] - m * me + 2 + n, n), m + 3)]
                for s in range(3)
            ] + [upper[i // 2]]
            below[i] = dot(wf[row], jnp.concatenate(parts, axis=0)).astype(BF16)
        upper = below

    forwards = []
    for k in range(1, R // 2):
        other = lax.rem(me + 2 * k, R)
        gather_copy(other, me, k).wait_recv()
        copy = gather_copy(other, twin, R // 2 + k)
        copy.start()
        forwards.append(copy)

    for pair in edges:
        for copy in pair:
            copy.wait_recv()
    part[0] = (edge_sum[0] + near_term(0, -1)).astype(BF16)
    part[count - 1] = (edge_sum[1] + near_term(count - 1, 1)).astype(BF16)

    for k in range(R // 2):
        other = lax.rem(twin + 2 * k, R)
        gather_copy(other, me, 0).wait_recv()
    for k in range(1, T):
        other = lax.rem(z + k, T)
        theirs = wc.at[pl.ds(other * block, block)]

        @pl.when(other < coarse_blocks)
        def _():
            send(theirs, theirs, table_send.at[0], table_recv.at[other], me, other).wait_recv()

    def coarse(n, index):
        return cr[index] if n == R else cu[n - 4 + index]

    n = R // 2
    while n >= 4:
        for j in range(n):
            lifted = dot_t(transfer(2 * n + 2 * j), coarse(2 * n, 2 * j)) + dot_t(
                transfer(2 * n + 2 * j + 1), coarse(2 * n, 2 * j + 1)
            )
            cu[n - 4 + j] = lifted.astype(BF16)
        n //= 2
    n = 4
    value = None
    while n <= R:
        row = n + me // (R // n)
        if n == 4:
            value = dot(wc[row][:, :rank], coarse(n, far_coarse[0, row]))
        else:
            parts = [coarse(n, far_coarse[s, row]) for s in range(3)] + [value]
            value = dot(wc[row], jnp.concatenate(parts, axis=0))
        value = value.astype(BF16)
        n *= 2
    for i in range(2):
        top[i] = dot(transfer(2 * R + 2 * me + i), value).astype(BF16)

    @pl.when(z == pair_owner)
    def _():
        for k in range(1, T):
            pair_copy(k, z, lax.rem(z - k + T, T)).wait_send()

    @pl.when(z < coarse_blocks)
    def _():
        for k in range(1, T):
            table_copy(k, z, lax.rem(z - k + T, T)).wait_send()

    for copy in gathers + forwards + tables:
        copy.wait_send()
    for pair in halos + edges:
        for copy in pair:
            copy.wait_send()


def finish(part, tt, f, top, out_hbm, out, sem):
    count = part.shape[0]
    stores = []
    for t in range(count):
        moments = jnp.concatenate([f[t], top[t * top.shape[0] // count]], axis=0)
        out[t] = (part[t].astype(F32) + dot(tt[t], moments)).astype(BF16)
        copy = pltpu.make_async_copy(out.at[t], out_hbm.at[t], sem.at[t])
        copy.start()
        stores.append(copy)
    for copy in stores:
        copy.wait()


def body(
    sources,
    near_blocks,
    near_list,
    source_basis,
    target_basis,
    transfer_fine,
    transfer_coarse,
    couple_fine,
    couple_coarse,
    far_fine,
    far_coarse,
):
    count, _, leaf, _ = near_blocks.shape
    rank = source_basis.shape[2]
    width = sources.shape[1]
    R, T = lax.axis_size("rows"), lax.axis_size("rhs")
    fine = transfer_fine.shape[0]
    block = transfer_coarse.shape[0]
    cuts = [1, 1 + (count - 2) // 4, count // 2, count - 1 - (count - 2) // 4, count - 1]
    spans = list(zip(cuts[:-1], cuts[1:]))
    pieces = 4
    dims = (count, leaf, rank, R, T, spans, pieces)
    hbm = pl.BlockSpec(memory_space=pltpu.HBM)
    vmem = pl.BlockSpec(memory_space=pltpu.VMEM)

    def in_hbm(a):
        return pltpu.with_memory_space_constraint(a, pltpu.HBM)

    def moments(clusters):
        return pltpu.VMEM((clusters, rank, width), BF16)

    dma = pltpu.SemaphoreType.DMA
    target = in_hbm(jnp.swapaxes(target_basis, 1, 2))
    results = pl.pallas_call(
        lambda *refs: kernel(dims, *refs),
        name="tree_apply",
        out_shape=[
            pltpu.VMEM((count, leaf, width), BF16),
            pltpu.VMEM((count, leaf, 2 * rank), BF16),
            moments(count),
            moments(count // 8),
        ],
        in_specs=[hbm] * 11,
        out_specs=[vmem] * 4,
        scratch_shapes=[
            pltpu.SMEM(near_list.shape[::-1], jnp.int32),
            pltpu.SMEM(far_fine.shape[::-1], jnp.int32),
            pltpu.SMEM(far_coarse.shape[::-1], jnp.int32),
            pltpu.VMEM((count + 2, leaf, width), BF16),
            pltpu.VMEM(near_blocks.shape, BF16),
            pltpu.VMEM((count, rank, leaf), BF16),
            pltpu.VMEM((count, rank, leaf), BF16),
            pltpu.VMEM(transfer_fine.shape, BF16),
            pltpu.VMEM(transfer_coarse.shape, BF16),
            pltpu.VMEM(couple_fine.shape, BF16),
            pltpu.VMEM(couple_coarse.shape, BF16),
            pltpu.VMEM((fine, rank, 4 * rank), BF16),
            pltpu.VMEM((block * T, rank, 4 * rank), BF16),
            moments(count + 4),
            moments(count // 2 + 4),
            moments(count // 4 + 4),
            moments(count // 8 + 4),
            moments(R),
            moments(R),
            moments(count // 8),
            moments(count // 4),
            moments(count // 2),
            pltpu.VMEM((2, leaf, width), F32),
            pltpu.VMEM((4, 2 * rank, 4 * rank), BF16),
            pltpu.VMEM((count // 2, rank, rank), BF16),
            pltpu.VMEM((count, rank, rank), BF16),
            dma((16 + len(spans),)),
            dma((2 * pieces,)),
            dma((2 * pieces,)),
            dma((8,)),
            dma((8,)),
            dma((T,)),
            dma((T,)),
            dma((R,)),
            dma((R,)),
            dma((T,)),
            dma((T,)),
            dma((2,)),
            dma((2,)),
            pltpu.SemaphoreType.REGULAR,
        ],
        compiler_params=pltpu.CompilerParams(
            collective_id=0, has_side_effects=True, vmem_limit_bytes=40 * MIB
        ),
    )(
        in_hbm(sources.reshape(count, leaf, width)),
        in_hbm(near_blocks),
        in_hbm(near_list.T),
        in_hbm(jnp.swapaxes(source_basis, 1, 2)),
        target,
        in_hbm(transfer_fine),
        in_hbm(transfer_coarse),
        in_hbm(couple_fine),
        in_hbm(couple_coarse),
        in_hbm(far_fine.T),
        in_hbm(far_coarse.T),
    )
    out = pl.pallas_call(
        finish,
        name="far_add",
        out_shape=jax.ShapeDtypeStruct((count, leaf, width), BF16),
        in_specs=[vmem] * 4,
        out_specs=pl.BlockSpec(memory_space=pl.ANY),
        scratch_shapes=[pltpu.VMEM((count, leaf, width), BF16), dma((count,))],
        compiler_params=pltpu.CompilerParams(vmem_limit_bytes=20 * MIB),
    )(*results)
    return out.reshape(count * leaf, width)


def solution(mesh):
    in_specs = (
        P("rows", "rhs"),
        P("rows", None, None, None),
        P("rows", None),
        P("rows", None, None),
        P("rows", None, None),
        P("rows", None, None),
        P("rhs", None, None),
        P("rows", None, None, None),
        P("rhs", None, None, None),
        P("rows", None),
        P(),
    )
    out_specs = P("rows", "rhs")
    return jax.shard_map(body, mesh=mesh, in_specs=in_specs, out_specs=out_specs, check_vma=False)
```

time: 29.6 us -> 21.6 us (0.73)
  the two profiles are of different devices: /device:TPU:0 before, /device:TPU:1 now
where the time goes in v1:
time: 21.6 us; the launch traced here: 21.5 us
  Pallas kernels  21.5 us (100%)
    pallas_call x1, Pallas kernels, body(): pl.pallas_call(lambda *refs: kernel(dims, *refs), name='tree_apply', out_...  19.1 us
    pallas_call x1, Pallas kernels, body(): pl.pallas_call(finish, name='far_add', out_shape=jax.ShapeDtypeStruct((co...  2.34 us

profile of v1, /device:TPU:1, one launch (start us, length us, event | category | flops | bytes accessed | tf_op | source)
XLA Modules:
  0.0 21.5 jit_solution(9425313908672088048)
XLA Ops:
  0.0 19.1 %tree_apply.1 = (bf16[16,256,512]{2,1,0:T(8,128)(2,1)S(1)}, bf16[16,256,64]{2,1,0:T(8,128)(2,1)S(1)}, bf16[16,32,512]{2,1,0:T(8,128)(2,1)S(1)}, bf16[2,32,512]{2,1,0:T(8,128)(2,1)S(1)}) custom-call(bf16[16,256,512]{2,1,0:T(8,128)(2,1)} %bitcast.7, bf16[16,3,256,256]{3,2,1,0:T(8,128)(2,1)} %refs_1_.1, s32[3,16]{1,0:T(4,128)} %bitcast.10, ...), custom_call_target="tpu_custom_call" | custom-call | tf_op jit(solution)/shard_map/tree_apply/pallas_call | solution.py:499
  19.1 2.3 %far_add.1 = bf16[16,256,512]{2,1,0:T(8,128)(2,1)} custom-call(bf16[16,256,512]{2,1,0:T(8,128)(2,1)S(1)} %get-tuple-element.9.part, bf16[16,256,64]{2,1,0:T(8,128)(2,1)S(1)} %get-tuple-element.10.tt, bf16[16,32,512]{2,1,0:T(8,128)(2,1)S(1)} %get-tuple-element.11.f, bf16[2,32,512]{2,1,0:T(8,128)(2,1)S(1)} %get-tuple-element.12.top), custom_call_target="tpu_custom_call" | custom-call | tf_op jit(solution)/shard_map/far_add/pallas_call | solution.py:568

commit v2 on v1

v2 whole, which is shorter than its diff:
```python
import jax
import jax.numpy as jnp
from jax import lax
from jax.experimental import pallas as pl
from jax.experimental.pallas import tpu as pltpu
from jax.sharding import PartitionSpec as P

MESH = pl.DeviceIdType.MESH
F32 = jnp.float32
BF16 = jnp.bfloat16
MIB = 1024 * 1024


def dot(a, b):
    return lax.dot_general(a, b, (((1,), (0,)), ((), ())), preferred_element_type=F32)


def dot_t(a, b):
    return lax.dot_general(a, b, (((0,), (0,)), ((), ())), preferred_element_type=F32)


def kernel(
    dims,
    x_hbm,
    near_hbm,
    near_list_hbm,
    sb_hbm,
    tb_hbm,
    ef_hbm,
    ec_hbm,
    sf_hbm,
    sc_hbm,
    far_fine_hbm,
    far_coarse_hbm,
    part,
    tt,
    f0,
    top,
    near_list,
    far_fine,
    far_coarse,
    xw,
    nears,
    near_edges,
    sb,
    tb,
    ef,
    sf,
    coarse_in,
    wf,
    wc,
    cw0,
    cw1,
    cw2,
    cw3,
    cr,
    cu,
    f3,
    f2,
    f1,
    edge_sum,
    lifts,
    q1,
    q0,
    load_sem,
    sent,
    edge_recv,
    halo_recv,
    table_recv,
    gather_recv,
    pair_recv,
    hello,
):
    count, leaf, rank, R, T, spans, pieces = dims
    me = lax.axis_index("rows")
    z = lax.axis_index("rhs")
    right, left = lax.rem(me + 1, R), lax.rem(me + R - 1, R)
    parity = lax.rem(me, 2)
    twin = me + 1 - 2 * parity
    block = coarse_in.shape[0]
    sizes = [count, count // 2, count // 4, count // 8]
    firsts = [0, count, count + count // 2]
    windows = [cw0, cw1, cw2, cw3]

    def whole(ref, sem):
        return pltpu.make_async_copy(ref, ref, sem)

    def load(source, target, k):
        copy = pltpu.make_async_copy(source, target, load_sem.at[k])
        copy.start()
        return copy

    barrier = pltpu.get_barrier_semaphore()
    for k in range(1, R):
        other = lax.rem(me + k, R)

        @pl.when((other > me) | (k in (1, R - 1)))
        def _():
            pl.semaphore_signal(barrier, inc=1, device_id=(other, z), device_id_type=MESH)

    for k in range(1, T):

        @pl.when(z + k < T)
        def _():
            pl.semaphore_signal(barrier, inc=1, device_id=(me, z + k), device_id_type=MESH)

    load(x_hbm.at[pl.ds(0, 1)], xw.at[pl.ds(1, 1)], 0)
    load(x_hbm.at[pl.ds(count - 1, 1)], xw.at[pl.ds(count, 1)], 0)
    load(ec_hbm, coarse_in.at[:, 3], 1)
    load(sc_hbm, coarse_in.at[:, pl.ds(0, 3)], 1)
    load_sb = load(sb_hbm, sb, 2)
    x_loads = [
        load(x_hbm.at[pl.ds(a, b - a)], xw.at[pl.ds(1 + a, b - a)], 7 + c)
        for c, (a, b) in enumerate(spans)
    ]
    load_ef = load(ef_hbm, ef, 3)
    load_lists = [
        load(near_list_hbm, near_list, 4),
        load(far_fine_hbm, far_fine, 5),
        load(far_coarse_hbm, far_coarse, 6),
    ]

    def send(src, dst, send_sem, recv_sem, row, col):
        return pltpu.make_async_remote_copy(
            src_ref=src,
            dst_ref=dst,
            send_sem=send_sem,
            recv_sem=recv_sem,
            device_id=(row, col),
            device_id_type=MESH,
        )

    def both(low_src, low_dst, high_src, high_dst, level):
        send(low_src, low_dst, sent.at[1], halo_recv.at[level], left, z).start()
        send(high_src, high_dst, sent.at[1], halo_recv.at[level], right, z).start()

    before = me - jnp.where(me > 0, 1, 0) - jnp.where(me == R - 1, 1, 0)
    pl.semaphore_wait(barrier, z + 2 + before)
    for k in range(2, R - 1):
        other = lax.rem(me + k, R)

        @pl.when(other < me)
        def _():
            pl.semaphore_signal(hello.at[0], inc=1, device_id=(other, z), device_id_type=MESH)

    for k in range(1, T):

        @pl.when(z >= k)
        def _():
            pl.semaphore_signal(hello.at[1], inc=1, device_id=(me, z - k), device_id_type=MESH)

    rows = leaf // pieces

    def edge_piece(k, source, first, last):
        span = pl.ds(k * rows, rows)
        low = send(
            source.at[first, span],
            xw.at[count + 1, span],
            sent.at[0],
            edge_recv.at[0],
            left,
            z,
        )
        high = send(
            source.at[last, span],
            xw.at[0, span],
            sent.at[0],
            edge_recv.at[0],
            right,
            z,
        )
        return [low, high]

    edges = [edge_piece(k, x_hbm, 0, count - 1) for k in range(pieces // 2)]
    for pair in edges:
        for copy in pair:
            copy.start()

    whole(coarse_in, load_sem.at[1]).wait()
    for r in range(block):
        wc[z * block + r] = jnp.concatenate([coarse_in[r, k] for k in range(4)], axis=1)
    compact = R == 8
    step = 1 - 2 * parity
    near_by = lax.rem(me - step + R, R)
    pair_owner = (2 * R + 2 * me) // block
    by_owner = (2 * R + 2 * near_by) // block
    coarse_blocks = (2 * R + block - 1) // block
    mine = wc.at[pl.ds(z * block, block)]

    def pair_copy(target):
        rows = wc.at[pl.ds(2 * R + 2 * me, 2)]
        return send(rows, rows, sent.at[2], pair_recv.at[0], me, target)

    def by_copy(target):
        rows = wc.at[pl.ds(2 * R + 2 * near_by, 2)]
        return send(rows, rows, sent.at[3], pair_recv.at[1], me, target)

    pair_copies = [(pair_owner, pair_copy)] + ([(by_owner, by_copy)] if compact else [])

    def table_copy(source, target):
        spot = jnp.minimum(source, coarse_blocks - 1)
        return send(mine, mine, sent.at[4], table_recv.at[spot], me, target)

    for owner, copy_of in pair_copies:

        @pl.when(z == owner)
        def _():
            for k in range(1, T):

                @pl.when(z >= k)
                def _():
                    copy_of(z - k).start()

    @pl.when((z > 0) & (z < coarse_blocks))
    def _():
        for k in range(1, T):

            @pl.when(z >= k)
            def _():
                table_copy(z, z - k).start()

    load_sb.wait()

    def leaf_moment(t):
        cw0[2 + t] = dot(sb[t], xw[1 + t]).astype(BF16)

    near_loads = []

    def load_near(c):
        if c < len(spans):
            span = pl.ds(spans[c][0], spans[c][1] - spans[c][0])
            return [load(near_hbm.at[span], nears[c], 7 + c)]
        return [
            load(near_hbm.at[pl.ds(t, 1)], near_edges.at[pl.ds(k, 1)], 0)
            for k, t in enumerate((0, count - 1))
        ]

    whole(xw.at[pl.ds(0, 2)], load_sem.at[0]).wait()
    leaf_moment(0)
    leaf_moment(count - 1)
    for c, (a, b) in enumerate(spans):
        x_loads[c].wait()
        near_loads.append(load_near(c))
        for t in range(a, b):
            leaf_moment(t)
    near_loads.append(load_near(len(spans)))
    load_sf = load(sf_hbm, sf, 2)
    load_tb = load(tb_hbm, tb, 1)

    early = (z == pair_owner) | (z == by_owner) if compact else z == pair_owner

    def hear_planes():
        @pl.when(z < T - 1)
        def _():
            pl.semaphore_wait(hello.at[1], T - 1 - z)

    @pl.when(early)
    def _():
        hear_planes()
        for owner, copy_of in pair_copies:

            @pl.when(z == owner)
            def _():
                for k in range(1, T):

                    @pl.when(z < T - k)
                    def _():
                        copy_of(z + k).start()

    load_ef.wait()

    def pair_matrix(level, j):
        first = firsts[level] + 2 * j
        return ef[first : first + 2].reshape(2 * rank, rank)

    low_pack = [pair_matrix(level, 0) for level in range(3)]
    high_pack = [pair_matrix(level, sizes[level + 1] - 1) for level in range(3)]
    lifts[0] = jnp.concatenate(low_pack + low_pack[:1], axis=1)
    lifts[1] = jnp.concatenate(high_pack + high_pack[:1], axis=1)

    for level in range(3):
        below, above = windows[level], windows[level + 1]
        for j in range(sizes[level + 1]):
            pair = below[2 + 2 * j : 4 + 2 * j].reshape(2 * rank, -1)
            above[2 + j] = dot_t(pair_matrix(level, j), pair).astype(BF16)
        if level == 0:
            both(lifts.at[0], lifts.at[3], lifts.at[1], lifts.at[2], 0)
            both(
                cw0.at[pl.ds(2, 2)],
                cw0.at[pl.ds(2 + count, 2)],
                cw0.at[pl.ds(count, 2)],
                cw0.at[pl.ds(0, 2)],
                0,
            )

    def inner_halo(level):
        ref, size = windows[level], sizes[level]
        both(
            ref.at[pl.ds(3, 1)],
            ref.at[pl.ds(size + 3, 1)],
            ref.at[pl.ds(size, 1)],
            ref.at[pl.ds(0, 1)],
            level,
        )

    for level in (1, 2, 3):
        inner_halo(level)

    for copy in load_lists:
        copy.wait()
    total = count * R

    def near_terms(t, near, at, first, last):
        blocks = []
        for wanted in range(first, last + 1):
            target = lax.rem(me * count + t + wanted + total, total)
            slot = jnp.where(
                near_list[0, t] == target, 0, jnp.where(near_list[1, t] == target, 1, 2)
            )
            blocks.append(near[at, slot])
        points = xw[1 + t + first : 2 + t + last].reshape(-1, xw.shape[2])
        return dot(jnp.concatenate(blocks, axis=1), points)

    def near_span(c):
        near_loads[c][0].wait()
        for t in range(*spans[c]):
            part[t] = near_terms(t, nears[c], t - spans[c][0], -1, 1).astype(BF16)


    for c in range(len(spans) // 2):
        near_span(c)

    @pl.when(jnp.logical_not(early))
    def _():
        hear_planes()

    @pl.when(z < coarse_blocks)
    def _():
        for k in range(1, T):

            @pl.when(z < T - k)
            def _():
                table_copy(z, z + k).start()

    for c in range(len(spans) // 2, len(spans)):
        near_span(c)

    def transfer(row):
        return wc[row][:, 3 * rank :]

    def coarse_moment(cluster, at):
        lower, upper = transfer(2 * R + 2 * cluster), transfer(2 * R + 2 * cluster + 1)
        cr[cluster] = (dot_t(lower, cw3[at]) + dot_t(upper, cw3[at + 1])).astype(BF16)

    def gather_copy(source, target, k):
        spot = cr.at[pl.ds(source, 1)]
        return send(spot, spot, sent.at[5], gather_recv.at[k], target, z)

    later = R - 1 - me - jnp.where(me == 0, 2, jnp.where(me == R - 1, 0, 1))

    @pl.when(later > 0)
    def _():
        pl.semaphore_wait(hello.at[0], later)

    @pl.when(z != pair_owner)
    def _():
        pair_copy(lax.rem(z + 1, T)).wait_recv()

    coarse_moment(me, 2)

    def ring(offset):
        return lax.rem(me + offset + 2 * R, R)

    if compact:
        targets = [(ring(2 * step), 0), (ring(R // 2), 1), (ring(R // 2 + step), 1)]
    else:
        targets = [(ring(2 * k), me) for k in range(1, R // 2)] + [(twin, me)]
    for target, k in targets:
        gather_copy(me, target, k).start()

    whole(near_edges, load_sem.at[0]).wait()
    edge_sum[0] = near_terms(0, near_edges, 0, 0, 1)
    edge_sum[1] = near_terms(count - 1, near_edges, 1, -1, 0)
    late = [edge_piece(k, xw, 1, count) for k in range(pieces // 2, pieces)]
    for pair in late:
        for copy in pair:
            copy.start()

    load_sf.wait()
    for j in range(wf.shape[0]):
        wf[j] = jnp.concatenate([sf[j, 0], sf[j, 1], sf[j, 2], ef[j]], axis=1)

    for j in range(sizes[2]):
        both_rows = dot(pair_matrix(1, j), ef[firsts[2] + j]).astype(BF16)
        q1[2 * j : 2 * j + 2] = both_rows.reshape(2, rank, rank)
    for j in range(sizes[1]):
        both_rows = dot(pair_matrix(0, j), q1[j]).astype(BF16)
        q0[2 * j : 2 * j + 2] = both_rows.reshape(2, rank, rank)
    across = lax.broadcasted_iota(jnp.int32, (rank, rank), 0)
    down = lax.broadcasted_iota(jnp.int32, (rank, rank), 1)
    unit = jnp.where(across == down, 1.0, 0.0).astype(BF16)
    load_tb.wait()
    for t in range(count):
        tt[t] = dot_t(tb[t], jnp.concatenate([unit, q0[t]], axis=1)).astype(BF16)

    whole(cw0.at[pl.ds(0, 5)], halo_recv.at[0]).wait()
    for level in range(3):
        below, above = windows[level], windows[level + 1]
        size = sizes[level]
        whole(cw0.at[pl.ds(0, 2)], halo_recv.at[level + 1]).wait()
        from_left = lifts[2][:, level * rank : (level + 1) * rank]
        from_right = lifts[3][:, level * rank : (level + 1) * rank]
        low_pair = below[0:2].reshape(2 * rank, -1)
        high_pair = below[size + 2 : size + 4].reshape(2 * rank, -1)
        above[1] = dot_t(from_left, low_pair).astype(BF16)
        above[size // 2 + 2] = dot_t(from_right, high_pair).astype(BF16)

    if compact:

        @pl.when(z != by_owner)
        def _():
            by_copy(lax.rem(z + 1, T)).wait_recv()

        coarse_moment(near_by, 4 * parity)
        gather_copy(near_by, twin, 2).start()

    for i in range(2):
        row = 2 * R + 2 * me + i
        parts = [
            cw3[jnp.minimum(lax.rem(far_coarse[s, row] - 2 * me + 2 + 2 * R, 2 * R), 5)]
            for s in range(3)
        ]
        f3[i] = dot(wc[row][:, : 3 * rank], jnp.concatenate(parts, axis=0)).astype(BF16)
    upper = f3
    for level, below in ((2, f2), (1, f1), (0, f0)):
        m = sizes[level]
        n = m * R
        for i in range(m):
            row = firsts[level] + i
            parts = [
                windows[level][jnp.minimum(lax.rem(far_fine[s, row] - m * me + 2 + n, n), m + 3)]
                for s in range(3)
            ] + [upper[i // 2]]
            below[i] = dot(wf[row], jnp.concatenate(parts, axis=0)).astype(BF16)
        upper = below

    if compact:
        beyond = ring(-2 * step)
        gather_copy(beyond, me, 0).wait_recv()
        gather_copy(beyond, twin, 2).start()
        whole(cr.at[pl.ds(0, 2)], gather_recv.at[1]).wait()
        whole(cr.at[pl.ds(0, 2)], gather_recv.at[2]).wait()
        passes = 5
    else:
        for k in range(1, R // 2):
            gather_copy(ring(2 * k), me, ring(2 * k)).wait_recv()
            gather_copy(ring(2 * k), twin, ring(2 * k)).start()
        for k in range(R // 2):
            other = lax.rem(twin + 2 * k, R)
            gather_copy(other, me, other).wait_recv()
        passes = R - 1
    for k in range(1, T):
        other = lax.rem(z + k, T)
        theirs = wc.at[pl.ds(other * block, block)]

        @pl.when(other < coarse_blocks)
        def _():
            spot = jnp.minimum(other, coarse_blocks - 1)
            send(theirs, theirs, sent.at[4], table_recv.at[spot], me, other).wait_recv()

    def coarse(n, index):
        return cr[index] if n == R else cu[n - 4 + index]

    def lift(n, j):
        lifted = dot_t(transfer(2 * n + 2 * j), coarse(2 * n, 2 * j)) + dot_t(
            transfer(2 * n + 2 * j + 1), coarse(2 * n, 2 * j + 1)
        )
        return lifted.astype(BF16)

    if not compact:
        n = R // 2
        while n >= 4:
            for j in range(n):
                cu[n - 4 + j] = lift(n, j)
            n //= 2
    n = 4
    value = None
    while n <= R:
        row = n + me // (R // n)
        if n == 4:
            opposite = lax.rem(me // (R // n) + 2, 4)
            moment = lift(4, opposite) if compact else coarse(4, opposite)
            value = dot(wc[row][:, :rank], moment)
        else:
            parts = [coarse(n, far_coarse[s, row]) for s in range(3)] + [value]
            value = dot(wc[row], jnp.concatenate(parts, axis=0))
        value = value.astype(BF16)
        n *= 2
    for i in range(2):
        top[i] = dot(transfer(2 * R + 2 * me + i), value).astype(BF16)

    whole(xw.at[pl.ds(0, 2)], edge_recv.at[0]).wait()
    part[0] = (edge_sum[0] + near_terms(0, near_edges, 0, -1, -1)).astype(BF16)
    part[count - 1] = (edge_sum[1] + near_terms(count - 1, near_edges, 1, 1, 1)).astype(BF16)

    for k, (owner, copy_of) in enumerate(pair_copies):

        @pl.when(z == owner)
        def _():
            whole(wc.at[pl.ds(0, 2 * (T - 1))], sent.at[2 + k]).wait()

    @pl.when(z < coarse_blocks)
    def _():
        whole(wc.at[pl.ds(0, block * (T - 1))], sent.at[4]).wait()

    whole(cr.at[pl.ds(0, passes)], sent.at[5]).wait()
    whole(xw.at[pl.ds(0, 2)], sent.at[0]).wait()
    whole(cw0.at[pl.ds(0, 11)], sent.at[1]).wait()


def finish(part, tt, f, top, out_hbm, out, sem):
    count = part.shape[0]
    for t in range(count):
        moments = jnp.concatenate([f[t], top[t * top.shape[0] // count]], axis=0)
        out[t] = (part[t].astype(F32) + dot(tt[t], moments)).astype(BF16)
        pltpu.make_async_copy(out.at[t], out_hbm.at[t], sem).start()
    pltpu.make_async_copy(out, out_hbm, sem).wait()


def body(
    sources,
    near_blocks,
    near_list,
    source_basis,
    target_basis,
    transfer_fine,
    transfer_coarse,
    couple_fine,
    couple_coarse,
    far_fine,
    far_coarse,
):
    count, _, leaf, _ = near_blocks.shape
    rank = source_basis.shape[2]
    width = sources.shape[1]
    R, T = lax.axis_size("rows"), lax.axis_size("rhs")
    fine = transfer_fine.shape[0]
    block = transfer_coarse.shape[0]
    cuts = [1, 1 + (count - 2) // 4, count // 2, count - 1 - (count - 2) // 4, count - 1]
    spans = list(zip(cuts[:-1], cuts[1:]))
    pieces = 4
    dims = (count, leaf, rank, R, T, spans, pieces)
    hbm = pl.BlockSpec(memory_space=pltpu.HBM)
    vmem = pl.BlockSpec(memory_space=pltpu.VMEM)

    def in_hbm(a):
        return pltpu.with_memory_space_constraint(a, pltpu.HBM)

    def moments(clusters):
        return pltpu.VMEM((clusters, rank, width), BF16)

    dma = pltpu.SemaphoreType.DMA
    target = in_hbm(jnp.swapaxes(target_basis, 1, 2))
    results = pl.pallas_call(
        lambda *refs: kernel(dims, *refs),
        name="tree_apply",
        out_shape=[
            pltpu.VMEM((count, leaf, width), BF16),
            pltpu.VMEM((count, leaf, 2 * rank), BF16),
            moments(count),
            moments(count // 8),
        ],
        in_specs=[hbm] * 11,
        out_specs=[vmem] * 4,
        scratch_shapes=[
            pltpu.SMEM(near_list.shape[::-1], jnp.int32),
            pltpu.SMEM(far_fine.shape[::-1], jnp.int32),
            pltpu.SMEM(far_coarse.shape[::-1], jnp.int32),
            pltpu.VMEM((count + 2, leaf, width), BF16),
            [pltpu.VMEM((b - a,) + near_blocks.shape[1:], BF16) for a, b in spans],
            pltpu.VMEM((2,) + near_blocks.shape[1:], BF16),
            pltpu.VMEM((count, rank, leaf), BF16),
            pltpu.VMEM((count, rank, leaf), BF16),
            pltpu.VMEM(transfer_fine.shape, BF16),
            pltpu.VMEM(couple_fine.shape, BF16),
            pltpu.VMEM((block, 4, rank, rank), BF16),
            pltpu.VMEM((fine, rank, 4 * rank), BF16),
            pltpu.VMEM((block * T, rank, 4 * rank), BF16),
            moments(count + 4),
            moments(count // 2 + 4),
            moments(count // 4 + 4),
            moments(count // 8 + 4),
            moments(R),
            moments(R),
            moments(count // 8),
            moments(count // 4),
            moments(count // 2),
            pltpu.VMEM((2, leaf, width), F32),
            pltpu.VMEM((4, 2 * rank, 4 * rank), BF16),
            pltpu.VMEM((count // 2, rank, rank), BF16),
            pltpu.VMEM((count, rank, rank), BF16),
            dma((7 + len(spans),)),
            dma((6,)),
            dma((1,)),
            dma((4,)),
            dma((2 * R // block,)),
            dma((3 if R == 8 else R,)),
            dma((2,)),
            pltpu.SemaphoreType.REGULAR((2,)),
        ],
        compiler_params=pltpu.CompilerParams(
            collective_id=0, has_side_effects=True, vmem_limit_bytes=40 * MIB
        ),
    )(
        in_hbm(sources.reshape(count, leaf, width)),
        in_hbm(near_blocks),
        in_hbm(near_list.T),
        in_hbm(jnp.swapaxes(source_basis, 1, 2)),
        target,
        in_hbm(transfer_fine),
        in_hbm(transfer_coarse),
        in_hbm(couple_fine),
        in_hbm(couple_coarse),
        in_hbm(far_fine.T),
        in_hbm(far_coarse.T),
    )
    out = pl.pallas_call(
        finish,
        name="far_add",
        out_shape=jax.ShapeDtypeStruct((count, leaf, width), BF16),
        in_specs=[vmem] * 4,
        out_specs=pl.BlockSpec(memory_space=pl.ANY),
        scratch_shapes=[pltpu.VMEM((count, leaf, width), BF16), dma],
        compiler_params=pltpu.CompilerParams(vmem_limit_bytes=20 * MIB),
    )(*results)
    return out.reshape(count * leaf, width)


def solution(mesh):
    in_specs = (
        P("rows", "rhs"),
        P("rows", None, None, None),
        P("rows", None),
        P("rows", None, None),
        P("rows", None, None),
        P("rows", None, None),
        P("rhs", None, None),
        P("rows", None, None, None),
        P("rhs", None, None, None),
        P("rows", None),
        P(),
    )
    out_specs = P("rows", "rhs")
    return jax.shard_map(body, mesh=mesh, in_specs=in_specs, out_specs=out_specs, check_vma=False)
```

time: 21.6 us -> 18.2 us (0.84); the launches traced: 21.5 us -> 17.8 us
  Pallas kernels: 21.5 us -> 17.8 us
    pallas_call x1, Pallas kernels: 19.1 us -> 15.6 us  [body(): pl.pallas_call(lambda *refs: kernel(dims, *refs), name='tree_apply', out_...]
where the time goes in v2:
time: 18.2 us; the launch traced here: 17.8 us
  Pallas kernels  17.8 us (98%)
    pallas_call x1, Pallas kernels, body(): pl.pallas_call(lambda *refs: kernel(dims, *refs), name='tree_apply', out_...  15.6 us
    pallas_call x1, Pallas kernels, body(): pl.pallas_call(finish, name='far_add', out_shape=jax.ShapeDtypeStruct((co...  2.2 us

profile of v2, /device:TPU:1, one launch (start us, length us, event | category | flops | bytes accessed | tf_op | source)
XLA Modules:
  0.0 17.8 jit_solution(10448696798413768924)
XLA Ops:
  0.0 15.6 %tree_apply.1 = (bf16[16,256,512]{2,1,0:T(8,128)(2,1)S(1)}, bf16[16,256,64]{2,1,0:T(8,128)(2,1)S(1)}, bf16[16,32,512]{2,1,0:T(8,128)(2,1)S(1)}, bf16[2,32,512]{2,1,0:T(8,128)(2,1)S(1)}) custom-call(bf16[16,256,512]{2,1,0:T(8,128)(2,1)} %bitcast.7, bf16[16,3,256,256]{3,2,1,0:T(8,128)(2,1)} %refs_1_.1, s32[3,16]{1,0:T(4,128)} %bitcast.10, ...), custom_call_target="tpu_custom_call" | custom-call | tf_op jit(solution)/shard_map/tree_apply/pallas_call | solution.py:564
  15.6 2.2 %far_add.1 = bf16[16,256,512]{2,1,0:T(8,128)(2,1)} custom-call(bf16[16,256,512]{2,1,0:T(8,128)(2,1)S(1)} %get-tuple-element.9.part, bf16[16,256,64]{2,1,0:T(8,128)(2,1)S(1)} %get-tuple-element.10.tt, bf16[16,32,512]{2,1,0:T(8,128)(2,1)S(1)} %get-tuple-element.11.f, bf16[2,32,512]{2,1,0:T(8,128)(2,1)S(1)} %get-tuple-element.12.top), custom_call_target="tpu_custom_call" | custom-call | tf_op jit(solution)/shard_map/far_add/pallas_call | solution.py:627

commit v3 on v2

v3 whole, which is shorter than its diff:
```python
import jax
import jax.numpy as jnp
from jax import lax
from jax.experimental import pallas as pl
from jax.experimental.pallas import tpu as pltpu
from jax.sharding import PartitionSpec as P

MESH = pl.DeviceIdType.MESH
F32 = jnp.float32
BF16 = jnp.bfloat16
LEAD = 6
MIB = 1024 * 1024


def dot(a, b):
    return lax.dot_general(a, b, (((1,), (0,)), ((), ())), preferred_element_type=F32)


def dot_n(a, b):
    return lax.dot_general(a, b, (((1,), (1,)), ((), ())), preferred_element_type=F32)


def dot_t(a, b):
    return lax.dot_general(a, b, (((0,), (0,)), ((), ())), preferred_element_type=F32)


def kernel(
    dims,
    x_hbm,
    near_hbm,
    near_list_hbm,
    sb_hbm,
    tb_hbm,
    ef_hbm,
    ec_hbm,
    sf_hbm,
    sc_hbm,
    far_fine_hbm,
    far_coarse_hbm,
    part,
    tt,
    f0,
    top,
    edge_block,
    beyond_leaf,
    near_list,
    far_fine,
    far_coarse,
    xw,
    nears,
    near_edges,
    sb,
    tb,
    ef,
    sf,
    coarse_in,
    wf,
    wc,
    cw0,
    cw1,
    cw2,
    cw3,
    cr,
    cu,
    f3,
    f2,
    f1,
    lifts,
    q1,
    q0,
    load_sem,
    sent,
    edge_recv,
    halo_recv,
    table_recv,
    gather_recv,
    rows_recv,
    hello,
):
    count, leaf, rank, R, T, spans = dims
    me = lax.axis_index("rows")
    z = lax.axis_index("rhs")
    right, left = lax.rem(me + 1, R), lax.rem(me + R - 1, R)
    parity = lax.rem(me, 2)
    twin = me + 1 - 2 * parity
    block = coarse_in.shape[0]
    compact = R == 8
    halo_sent, gather_sent, rows_sent = (0, 0, 1) if compact else (1, 2, 4)
    sizes = [count, count // 2, count // 4, count // 8]
    firsts = [0, count, count + count // 2]
    windows = [cw0, cw1, cw2, cw3]

    def whole(ref, sem):
        return pltpu.make_async_copy(ref, ref, sem)

    def load(source, target, k):
        copy = pltpu.make_async_copy(source, target, load_sem.at[k])
        copy.start()
        return copy

    barrier = pltpu.get_barrier_semaphore()
    for k in range(1, R):
        other = lax.rem(me + k, R)

        @pl.when((other > me) | (k in (1, R - 1)))
        def _():
            pl.semaphore_signal(barrier, inc=1, device_id=(other, z), device_id_type=MESH)

    for k in range(1, T):

        @pl.when(z + k < T)
        def _():
            pl.semaphore_signal(barrier, inc=1, device_id=(me, z + k), device_id_type=MESH)

    load(x_hbm.at[pl.ds(0, 1)], xw.at[pl.ds(1, 1)], 0)
    load(x_hbm.at[pl.ds(count - 1, 1)], xw.at[pl.ds(count, 1)], 0)
    load(ec_hbm, coarse_in.at[:, 3], 1)
    load(sc_hbm, coarse_in.at[:, pl.ds(0, 3)], 1)
    load_sb = load(sb_hbm, sb, 2)
    x_loads = [
        load(x_hbm.at[pl.ds(a, b - a)], xw.at[pl.ds(1 + a, b - a)], 7 + c)
        for c, (a, b) in enumerate(spans)
    ]
    load_ef = load(ef_hbm, ef, 3)
    load_lists = [
        load(near_list_hbm, near_list, 4),
        load(far_fine_hbm, far_fine, 5),
        load(far_coarse_hbm, far_coarse, 6),
    ]

    def send(src, dst, send_sem, recv_sem, row, col):
        return pltpu.make_async_remote_copy(
            src_ref=src,
            dst_ref=dst,
            send_sem=send_sem,
            recv_sem=recv_sem,
            device_id=(row, col),
            device_id_type=MESH,
        )

    def both(low_src, low_dst, high_src, high_dst, level):
        send(low_src, low_dst, sent.at[halo_sent], halo_recv.at[min(level, 1)], left, z).start()
        send(high_src, high_dst, sent.at[halo_sent], halo_recv.at[min(level, 1)], right, z).start()

    step = 1 - 2 * parity
    near_by = lax.rem(me - step + R, R)
    coarse_blocks = (2 * R + block - 1) // block
    mine = wc.at[pl.ds(z * block, block)]

    opposite = lax.rem(me // 2 + 2, 4)
    row_sets = [(2 * R + 2 * me, 2)]
    if compact:
        row_sets += [(2 * R + 2 * near_by, 2), (R + me, 1), (R + 2 * opposite, 2), (4 + me // 2, 1)]

    def rows_copy(k, target):
        first, size = row_sets[k]
        rows = wc.at[pl.ds(first, size)]
        return send(rows, rows, sent.at[rows_sent + k], rows_recv.at[k], me, target)

    def owner(k):
        return row_sets[k][0] // block

    def send_rows(chosen, before):
        for k in chosen:

            @pl.when(z == owner(k))
            def _():
                for d in range(1, T):
                    target = z - d if before else z + d

                    @pl.when((target >= 0) & (target < T))
                    def _():
                        rows_copy(k, target).start()

    def receive_rows(chosen):
        for k in chosen:

            @pl.when(z != owner(k))
            def _():
                rows_copy(k, lax.rem(z + 1, T)).wait_recv()

    def send_tables(before):
        if not compact:

            @pl.when(z < coarse_blocks)
            def _():
                for d in range(1, T):
                    target = z - d if before else z + d

                    @pl.when((target >= 0) & (target < T))
                    def _():
                        spot = table_recv.at[z]
                        send(mine, mine, sent.at[3], spot, me, target).start()

    urgent = range(min(2, len(row_sets)))
    later_sets = range(len(urgent), len(row_sets))
    early = (z == owner(0)) | (z == owner(urgent[-1]))

    cut = leaf * LEAD // 8
    outward = jnp.where(parity == 0, left, right)
    leads = jnp.where(me < 2, parity == 0, outward < lax.rem(me + 2 * step + R, R))

    def send_edge(source, first, high, begin=0, end=leaf):
        at = first + (count - 1 if high else 0)
        span = pl.ds(begin, end - begin)
        landing = beyond_leaf.at[0 if high else 1, span]
        target = right if high else left
        send(source.at[at, span], landing, sent.at[0], edge_recv.at[0], target, z).start()

    def enter():
        before = me - jnp.where(me > 0, 1, 0) - jnp.where(me == R - 1, 1, 0)
        pl.semaphore_wait(barrier, z + 2 + before)
        for k in range(2, R - 1):
            other = lax.rem(me + k, R)

            @pl.when(other < me)
            def _():
                pl.semaphore_signal(
                    hello.at[0], inc=1, device_id=(other, z), device_id_type=MESH
                )

        for k in range(1, T):

            @pl.when(z >= k)
            def _():
                pl.semaphore_signal(hello.at[1], inc=1, device_id=(me, z - k), device_id_type=MESH)

        for high in (0, 1):

            @pl.when(parity != high)
            def _():
                send_edge(x_hbm, 0, high)

            @pl.when(leads & (parity == high))
            def _():
                send_edge(x_hbm, 0, high, 0, cut)


    def coarse_rows():
        whole(coarse_in, load_sem.at[1]).wait()
        for r in range(block):
            wc[z * block + r] = jnp.concatenate([coarse_in[r, k] for k in range(4)], axis=1)
        send_rows(range(len(row_sets)), True)
        send_tables(True)

    def hear_planes():
        @pl.when(z < T - 1)
        def _():
            pl.semaphore_wait(hello.at[1], T - 1 - z)

    def early_rows():
        @pl.when(early)
        def _():
            hear_planes()
            send_rows(urgent, False)

    near_loads = [
        pltpu.make_async_copy(near_hbm.at[pl.ds(a, b - a)], nears[c], load_sem.at[7 + c])
        for c, (a, b) in enumerate(spans)
    ]
    edge_loads = [
        pltpu.make_async_copy(near_hbm.at[pl.ds(t, 1)], near_edges.at[pl.ds(k, 1)], load_sem.at[0])
        for k, t in enumerate((0, count - 1))
    ]
    load_sf = pltpu.make_async_copy(sf_hbm, sf, load_sem.at[2])
    load_tb = pltpu.make_async_copy(tb_hbm, tb, load_sem.at[1])

    def leaf_moment(t):
        cw0[2 + t] = dot(sb[t], xw[1 + t]).astype(BF16)

    def moments():
        load_sb.wait()
        whole(xw.at[pl.ds(0, 2)], load_sem.at[0]).wait()
        leaf_moment(0)
        leaf_moment(count - 1)
        for c, (a, b) in enumerate(spans):
            x_loads[c].wait()
            near_loads[c].start()
            for t in range(a, b):
                leaf_moment(t)
        for copy in edge_loads + [load_sf]:
            copy.start()

    def pair_matrix(level, j):
        first = firsts[level] + 2 * j
        return ef[first : first + 2].reshape(2 * rank, rank)

    def halo(level):
        ref, size = windows[level], sizes[level]
        if level == 0:
            both(lifts.at[0], lifts.at[3], lifts.at[1], lifts.at[2], 0)
        width, at = (2, 2) if level == 0 else (1, 3)
        both(
            ref.at[pl.ds(at, width)],
            ref.at[pl.ds(size + at, width)],
            ref.at[pl.ds(size, width)],
            ref.at[pl.ds(0, width)],
            level,
        )

    def upward(sending):
        load_ef.wait()
        low_pack = [pair_matrix(level, 0) for level in range(3)]
        high_pack = [pair_matrix(level, sizes[level + 1] - 1) for level in range(3)]
        lifts[0] = jnp.concatenate(low_pack + low_pack[:1], axis=1)
        lifts[1] = jnp.concatenate(high_pack + high_pack[:1], axis=1)
        for level in range(3):
            below, above = windows[level], windows[level + 1]
            for j in range(sizes[level + 1]):
                pair = below[2 + 2 * j : 4 + 2 * j].reshape(2 * rank, -1)
                above[2 + j] = dot_t(pair_matrix(level, j), pair).astype(BF16)
            if level == 0 and sending:
                halo(0)

    first_chip = (me < 2) & (z == 0)

    @pl.when(first_chip)
    def _():
        moments()
        upward(False)
        enter()
        halo(0)

    @pl.when(jnp.logical_not(first_chip))
    def _():
        enter()
        coarse_rows()
        moments()
        early_rows()
        upward(True)

    for level in (1, 2, 3):
        halo(level)

    @pl.when(first_chip)
    def _():
        coarse_rows()
        early_rows()

    load_tb.start()
    for copy in load_lists:
        copy.wait()
    total = count * R

    def near_block(t, near, at, wanted):
        target = lax.rem(me * count + t + wanted + total, total)
        slot = jnp.where(
            near_list[0, t] == target, 0, jnp.where(near_list[1, t] == target, 1, 2)
        )
        return near[at, slot]

    def near_terms(t, near, at, first, last):
        blocks = [near_block(t, near, at, wanted) for wanted in range(first, last + 1)]
        points = xw[1 + t + first : 2 + t + last].reshape(-1, xw.shape[2])
        return dot(jnp.concatenate(blocks, axis=1), points)

    def near_span(c):
        near_loads[c].wait()
        for t in range(*spans[c]):
            part[t] = near_terms(t, nears[c], t - spans[c][0], -1, 1).astype(BF16)


    for c in range(len(spans)):
        near_span(c)

    def transfer(row):
        return wc[row][:, 3 * rank :]

    def coarse_moment(cluster, at):
        lower, upper = transfer(2 * R + 2 * cluster), transfer(2 * R + 2 * cluster + 1)
        cr[cluster] = (dot_t(lower, cw3[at]) + dot_t(upper, cw3[at + 1])).astype(BF16)

    def gather_copy(source, target, k):
        spot = cr.at[pl.ds(source, 1)]
        return send(spot, spot, sent.at[gather_sent], gather_recv.at[k], target, z)

    @pl.when(jnp.logical_not(early))
    def _():
        hear_planes()

    send_rows(later_sets, False)
    send_tables(False)
    later = R - 1 - me - jnp.where(me == 0, 2, jnp.where(me == R - 1, 0, 1))

    @pl.when(later > 0)
    def _():
        pl.semaphore_wait(hello.at[0], later)

    receive_rows(range(1))
    coarse_moment(me, 2)

    def ring(offset):
        return lax.rem(me + offset + 2 * R, R)

    if compact:
        targets = [(ring(2 * step), 0), (ring(R // 2), 1), (ring(R // 2 + step), 1)]
    else:
        targets = [(ring(2 * k), me) for k in range(1, R // 2)] + [(twin, me)]
    for target, k in targets:
        gather_copy(me, target, k).start()

    for high in (0, 1):

        @pl.when(leads & (parity == high))
        def _():
            send_edge(xw, 1, high, cut, leaf)

    whole(near_edges, load_sem.at[0]).wait()
    part[0] = near_terms(0, near_edges, 0, 0, 1).astype(BF16)
    part[count - 1] = near_terms(count - 1, near_edges, 1, -1, 0).astype(BF16)
    edge_block[0] = near_block(0, near_edges, 0, -1)
    edge_block[1] = near_block(count - 1, near_edges, 1, 1)

    load_sf.wait()
    for j in range(wf.shape[0]):
        wf[j] = jnp.concatenate([sf[j, 0], sf[j, 1], sf[j, 2], ef[j]], axis=1)

    for j in range(sizes[2]):
        both_rows = dot(pair_matrix(1, j), ef[firsts[2] + j]).astype(BF16)
        q1[2 * j : 2 * j + 2] = both_rows.reshape(2, rank, rank)
    for j in range(sizes[1]):
        both_rows = dot(pair_matrix(0, j), q1[j]).astype(BF16)
        q0[2 * j : 2 * j + 2] = both_rows.reshape(2, rank, rank)
    across = lax.broadcasted_iota(jnp.int32, (rank, rank), 0)
    down = lax.broadcasted_iota(jnp.int32, (rank, rank), 1)
    unit = jnp.where(across == down, 1.0, 0.0).astype(BF16)
    load_tb.wait()
    for t in range(count):
        tt[t] = dot_t(tb[t], jnp.concatenate([unit, q0[t]], axis=1)).astype(BF16)

    for high in (0, 1):

        @pl.when(jnp.logical_not(leads | first_chip) & (parity == high))
        def _():
            send_edge(xw, 1, high)

    whole(cw0.at[pl.ds(0, 5)], halo_recv.at[0]).wait()
    for level in range(3):
        below, above = windows[level], windows[level + 1]
        size = sizes[level]
        if level == 0:
            whole(cw0.at[pl.ds(0, 6)], halo_recv.at[1]).wait()
        from_left = lifts[2][:, level * rank : (level + 1) * rank]
        from_right = lifts[3][:, level * rank : (level + 1) * rank]
        low_pair = below[0:2].reshape(2 * rank, -1)
        high_pair = below[size + 2 : size + 4].reshape(2 * rank, -1)
        above[1] = dot_t(from_left, low_pair).astype(BF16)
        above[size // 2 + 2] = dot_t(from_right, high_pair).astype(BF16)

    for high in (0, 1):

        @pl.when(jnp.logical_not(leads) & first_chip & (parity == high))
        def _():
            send_edge(xw, 1, high)

    if compact:

        receive_rows(range(1, 2))
        coarse_moment(near_by, 4 * parity)
        gather_copy(near_by, twin, 2).start()

    for i in range(2):
        row = 2 * R + 2 * me + i
        parts = [
            cw3[jnp.minimum(lax.rem(far_coarse[s, row] - 2 * me + 2 + 2 * R, 2 * R), 5)]
            for s in range(3)
        ]
        f3[i] = dot(wc[row][:, : 3 * rank], jnp.concatenate(parts, axis=0)).astype(BF16)
    upper = f3
    for level, below in ((2, f2), (1, f1), (0, f0)):
        m = sizes[level]
        n = m * R
        for i in range(m):
            row = firsts[level] + i
            parts = [
                windows[level][jnp.minimum(lax.rem(far_fine[s, row] - m * me + 2 + n, n), m + 3)]
                for s in range(3)
            ] + [upper[i // 2]]
            below[i] = dot(wf[row], jnp.concatenate(parts, axis=0)).astype(BF16)
        upper = below

    receive_rows(later_sets)
    if not compact:
        for k in range(1, T):
            other = lax.rem(z + k, T)
            theirs = wc.at[pl.ds(other * block, block)]

            @pl.when(other < coarse_blocks)
            def _():
                spot = table_recv.at[other]
                send(theirs, theirs, sent.at[3], spot, me, other).wait_recv()

    def upper_rows():
        return jnp.concatenate([transfer(2 * R + 2 * me + i) for i in range(2)], axis=0)

    if compact:
        down = dot(upper_rows(), wc[R + me]).astype(BF16)
        across = wc[4 + me // 2][:, :rank]
        lifted = [dot_n(across, transfer(R + 2 * opposite + i)).astype(BF16) for i in range(2)]
        far_up = dot(down[:, 3 * rank :], jnp.concatenate(lifted, axis=1)).astype(BF16)
        coarse_matrix = jnp.concatenate([down[:, : 3 * rank], far_up], axis=1)

    if compact:
        beyond = ring(-2 * step)
        gather_copy(beyond, me, 0).wait_recv()
        gather_copy(beyond, twin, 2).start()
        whole(cr.at[pl.ds(0, 2)], gather_recv.at[1]).wait()
        whole(cr.at[pl.ds(0, 2)], gather_recv.at[2]).wait()
        passes = 5
    else:
        for k in range(1, R // 2):
            gather_copy(ring(2 * k), me, ring(2 * k)).wait_recv()
            gather_copy(ring(2 * k), twin, ring(2 * k)).start()
        for k in range(R // 2):
            other = lax.rem(twin + 2 * k, R)
            gather_copy(other, me, other).wait_recv()
        passes = R - 1
    def coarse(n, index):
        return cr[index] if n == R else cu[n - 4 + index]

    def lift(n, j):
        lifted = dot_t(transfer(2 * n + 2 * j), coarse(2 * n, 2 * j)) + dot_t(
            transfer(2 * n + 2 * j + 1), coarse(2 * n, 2 * j + 1)
        )
        return lifted.astype(BF16)

    if compact:
        parts = [cr[far_coarse[s, R + me]] for s in range(3)]
        parts += [cr[2 * opposite], cr[2 * opposite + 1]]
        pair = dot(coarse_matrix, jnp.concatenate(parts, axis=0))
    else:
        n = R // 2
        while n >= 4:
            for j in range(n):
                cu[n - 4 + j] = lift(n, j)
            n //= 2
        n = 4
        value = None
        while n <= R:
            row = n + me // (R // n)
            if n == 4:
                value = dot(wc[row][:, :rank], coarse(n, far_coarse[0, row]))
            else:
                parts = [coarse(n, far_coarse[s, row]) for s in range(3)] + [value]
                value = dot(wc[row], jnp.concatenate(parts, axis=0))
            value = value.astype(BF16)
            n *= 2
        pair = dot(upper_rows(), value)
    top[...] = pair.astype(BF16).reshape(top.shape)

    whole(xw.at[pl.ds(0, 2)], edge_recv.at[0]).wait()
    for k in range(len(row_sets)):

        @pl.when(z == owner(k))
        def _():
            whole(wc.at[pl.ds(0, row_sets[k][1] * (T - 1))], sent.at[rows_sent + k]).wait()

    if not compact:

        @pl.when(z < coarse_blocks)
        def _():
            whole(wc.at[pl.ds(0, block * (T - 1))], sent.at[3]).wait()

    if compact:
        leaves, over = divmod(2 * leaf + (11 + passes) * rank, leaf)
        assert over == 0
        whole(xw.at[pl.ds(0, leaves)], sent.at[0]).wait()
    else:
        whole(xw.at[pl.ds(0, 2)], sent.at[0]).wait()
        whole(cw0.at[pl.ds(0, 11)], sent.at[halo_sent]).wait()
        whole(cr.at[pl.ds(0, passes)], sent.at[gather_sent]).wait()


def finish(part, tt, f, top, edge_block, beyond_leaf, out_hbm, out, sem):
    count = part.shape[0]
    middle = count // 2
    order = [*range(1, middle), 0, count - 1, *range(middle, count - 1)]
    for t in order:
        matrix, rows = tt[t], jnp.concatenate([f[t], top[t * top.shape[0] // count]], axis=0)
        if t in (0, count - 1):
            matrix = jnp.concatenate([edge_block[t // (count - 1)], matrix], axis=1)
            rows = jnp.concatenate([beyond_leaf[t // (count - 1)], rows], axis=0)
        out[t] = (part[t].astype(F32) + dot(matrix, rows)).astype(BF16)
        pltpu.make_async_copy(out.at[t], out_hbm.at[t], sem).start()
    pltpu.make_async_copy(out, out_hbm, sem).wait()


def body(
    sources,
    near_blocks,
    near_list,
    source_basis,
    target_basis,
    transfer_fine,
    transfer_coarse,
    couple_fine,
    couple_coarse,
    far_fine,
    far_coarse,
):
    count, _, leaf, _ = near_blocks.shape
    rank = source_basis.shape[2]
    width = sources.shape[1]
    R, T = lax.axis_size("rows"), lax.axis_size("rhs")
    fine = transfer_fine.shape[0]
    block = transfer_coarse.shape[0]
    cuts = [1, 1 + (count - 2) // 4, count // 2, count - 1 - (count - 2) // 4, count - 1]
    spans = list(zip(cuts[:-1], cuts[1:]))
    dims = (count, leaf, rank, R, T, spans)
    hbm = pl.BlockSpec(memory_space=pltpu.HBM)
    vmem = pl.BlockSpec(memory_space=pltpu.VMEM)

    def in_hbm(a):
        return pltpu.with_memory_space_constraint(a, pltpu.HBM)

    def moments(clusters):
        return pltpu.VMEM((clusters, rank, width), BF16)

    dma = pltpu.SemaphoreType.DMA
    target = in_hbm(jnp.swapaxes(target_basis, 1, 2))
    results = pl.pallas_call(
        lambda *refs: kernel(dims, *refs),
        name="tree_apply",
        out_shape=[
            pltpu.VMEM((count, leaf, width), BF16),
            pltpu.VMEM((count, leaf, 2 * rank), BF16),
            moments(count),
            moments(count // 8),
            pltpu.VMEM((2, leaf, leaf), BF16),
            pltpu.VMEM((2, leaf, width), BF16),
        ],
        in_specs=[hbm] * 11,
        out_specs=[vmem] * 6,
        scratch_shapes=[
            pltpu.SMEM(near_list.shape[::-1], jnp.int32),
            pltpu.SMEM(far_fine.shape[::-1], jnp.int32),
            pltpu.SMEM(far_coarse.shape[::-1], jnp.int32),
            pltpu.VMEM((count + 2, leaf, width), BF16),
            [pltpu.VMEM((b - a,) + near_blocks.shape[1:], BF16) for a, b in spans],
            pltpu.VMEM((2,) + near_blocks.shape[1:], BF16),
            pltpu.VMEM((count, rank, leaf), BF16),
            pltpu.VMEM((count, rank, leaf), BF16),
            pltpu.VMEM(transfer_fine.shape, BF16),
            pltpu.VMEM(couple_fine.shape, BF16),
            pltpu.VMEM((block, 4, rank, rank), BF16),
            pltpu.VMEM((fine, rank, 4 * rank), BF16),
            pltpu.VMEM((block * T, rank, 4 * rank), BF16),
            moments(count + 4),
            moments(count // 2 + 4),
            moments(count // 4 + 4),
            moments(count // 8 + 4),
            moments(R),
            moments(R),
            moments(count // 8),
            moments(count // 4),
            moments(count // 2),
            pltpu.VMEM((4, 2 * rank, 4 * rank), BF16),
            pltpu.VMEM((count // 2, rank, rank), BF16),
            pltpu.VMEM((count, rank, rank), BF16),
            dma((7 + len(spans),)),
            dma((6 if R == 8 else 5,)),
            dma((1,)),
            dma((2,)),
            dma((1 if R == 8 else T,)),
            dma((3 if R == 8 else R,)),
            dma((5 if R == 8 else 1,)),
            pltpu.SemaphoreType.REGULAR((2,)),
        ],
        compiler_params=pltpu.CompilerParams(
            collective_id=0, has_side_effects=True, vmem_limit_bytes=40 * MIB
        ),
    )(
        in_hbm(sources.reshape(count, leaf, width)),
        in_hbm(near_blocks),
        in_hbm(near_list.T),
        in_hbm(jnp.swapaxes(source_basis, 1, 2)),
        target,
        in_hbm(transfer_fine),
        in_hbm(transfer_coarse),
        in_hbm(couple_fine),
        in_hbm(couple_coarse),
        in_hbm(far_fine.T),
        in_hbm(far_coarse.T),
    )
    out = pl.pallas_call(
        finish,
        name="far_add",
        out_shape=jax.ShapeDtypeStruct((count, leaf, width), BF16),
        in_specs=[vmem] * 6,
        out_specs=pl.BlockSpec(memory_space=pl.ANY),
        scratch_shapes=[pltpu.VMEM((count, leaf, width), BF16), dma],
        compiler_params=pltpu.CompilerParams(vmem_limit_bytes=20 * MIB),
    )(*results)
    return out.reshape(count * leaf, width)


def solution(mesh):
    in_specs = (
        P("rows", "rhs"),
        P("rows", None, None, None),
        P("rows", None),
        P("rows", None, None),
        P("rows", None, None),
        P("rows", None, None),
        P("rhs", None, None),
        P("rows", None, None, None),
        P("rhs", None, None, None),
        P("rows", None),
        P(),
    )
    out_specs = P("rows", "rhs")
    return jax.shard_map(body, mesh=mesh, in_specs=in_specs, out_specs=out_specs, check_vma=False)
```

time: 18.2 us -> 17.1 us (0.940)
  Pallas kernels: 17.8 us -> 16.9 us
    pallas_call x1, Pallas kernels: 15.6 us -> 14.7 us  [body(): pl.pallas_call(lambda *refs: kernel(dims, *refs), name='tree_apply', out_...]
where the time goes in v3:
time: 17.1 us; the launch traced here: 16.9 us
  Pallas kernels  16.9 us (99%)
    pallas_call x1, Pallas kernels, body(): pl.pallas_call(lambda *refs: kernel(dims, *refs), name='tree_apply', out_...  14.7 us
    pallas_call x1, Pallas kernels, body(): pl.pallas_call(finish, name='far_add', out_shape=jax.ShapeDtypeStruct((co...  2.21 us

profile of v3, /device:TPU:1, one launch (start us, length us, event | category | flops | bytes accessed | tf_op | source)
XLA Modules:
  0.0 16.9 jit_solution(6266001460656780233)
XLA Ops:
  0.0 14.7 %tree_apply.1 = (bf16[16,256,512]{2,1,0:T(8,128)(2,1)S(1)}, bf16[16,256,64]{2,1,0:T(8,128)(2,1)S(1)}, bf16[16,32,512]{2,1,0:T(8,128)(2,1)S(1)}, bf16[2,32,512]{2...) custom-call(bf16[16,256,512]{2,1,0:T(8,128)(2,1)} %bitcast.7, ...), custom_call_target="tpu_custom_call" | custom-call | tf_op jit(solution)/shard_map/tree_apply/pallas_call | solution.py:621
  14.7 2.2 %far_add.1 = bf16[16,256,512]{2,1,0:T(8,128)(2,1)} custom-call(bf16[16,256,512]{2,1,0:T(8,128)(2,1)S(1)} %get-tuple-element.11.part, bf16[16,256,64]{2,1,0:T(8,128)(2,1)S(1)} %get-tuple-element.12.tt, bf16[16,32,512]{2,1,0:T(8,128)(2,1)S(1)} %get-tuple-element.13.f, bf16[2,32,512]{2,1,0:T(8,128)(2,1)S(1)} %get-tuple-element.14.top, ...), custom_call_target="tpu_custom_call" | custom-call | tf_op jit(solution)/shard_map/far_add/pallas_call | solution.py:685

commit v4 on v3

--- a/solution.py
+++ b/solution.py
@@ -9,6 +9,7 @@
 F32 = jnp.float32
 BF16 = jnp.bfloat16
 LEAD = 6
+TRAIL = 4
 MIB = 1024 * 1024
 
 
@@ -72,7 +73,6 @@
     sent,
     edge_recv,
     halo_recv,
-    table_recv,
     gather_recv,
     rows_recv,
     hello,
@@ -102,7 +102,7 @@
     for k in range(1, R):
         other = lax.rem(me + k, R)
 
-        @pl.when((other > me) | (k in (1, R - 1)))
+        @pl.when((k in (1, R - 1)) | ((other > me) & (not compact)))
         def _():
             pl.semaphore_signal(barrier, inc=1, device_id=(other, z), device_id_type=MESH)
 
@@ -189,7 +189,7 @@
 
                     @pl.when((target >= 0) & (target < T))
                     def _():
-                        spot = table_recv.at[z]
+                        spot = rows_recv.at[1 + z]
                         send(mine, mine, sent.at[3], spot, me, target).start()
 
     urgent = range(min(2, len(row_sets)))
@@ -198,7 +198,7 @@
 
     cut = leaf * LEAD // 8
     outward = jnp.where(parity == 0, left, right)
-    leads = jnp.where(me < 2, parity == 0, outward < lax.rem(me + 2 * step + R, R))
+    leads = jnp.where((me < 2) & (z == 0), parity == 0, outward < lax.rem(me + 2 * step + R, R))
 
     def send_edge(source, first, high, begin=0, end=leaf):
         at = first + (count - 1 if high else 0)
@@ -207,17 +207,37 @@
         target = right if high else left
         send(source.at[at, span], landing, sent.at[0], edge_recv.at[0], target, z).start()
 
+    rounds = [0, 2, 3]
+
+    def tell(k):
+        for other in (left, right):
+            pl.semaphore_signal(
+                hello.at[rounds[k]], inc=1, device_id=(other, z), device_id_type=MESH
+            )
+
+    def hear(k):
+        pl.semaphore_wait(hello.at[rounds[k]], 2)
+
+    def pass_on(k):
+        if compact:
+            hear(k)
+            tell(k + 1)
+
     def enter():
-        before = me - jnp.where(me > 0, 1, 0) - jnp.where(me == R - 1, 1, 0)
-        pl.semaphore_wait(barrier, z + 2 + before)
-        for k in range(2, R - 1):
-            other = lax.rem(me + k, R)
-
-            @pl.when(other < me)
-            def _():
-                pl.semaphore_signal(
-                    hello.at[0], inc=1, device_id=(other, z), device_id_type=MESH
-                )
+        if compact:
+            pl.semaphore_wait(barrier, z + 2)
+            tell(0)
+        else:
+            before = me - jnp.where(me > 0, 1, 0) - jnp.where(me == R - 1, 1, 0)
+            pl.semaphore_wait(barrier, z + 2 + before)
+            for k in range(2, R - 1):
+                other = lax.rem(me + k, R)
+
+                @pl.when(other < me)
+                def _():
+                    pl.semaphore_signal(
+                        hello.at[0], inc=1, device_id=(other, z), device_id_type=MESH
+                    )
 
         for k in range(1, T):
 
@@ -327,6 +347,7 @@
         coarse_rows()
         moments()
         early_rows()
+        pass_on(0)
         upward(True)
 
     for level in (1, 2, 3):
@@ -362,6 +383,18 @@
 
     for c in range(len(spans)):
         near_span(c)
+        if c == 0:
+
+            @pl.when(jnp.logical_not(first_chip))
+            def _():
+                pass_on(1)
+
+        if c < 2:
+
+            @pl.when(first_chip)
+            def _():
+                pass_on(c)
+
 
     def transfer(row):
         return wc[row][:, 3 * rank :]
@@ -380,11 +413,14 @@
 
     send_rows(later_sets, False)
     send_tables(False)
-    later = R - 1 - me - jnp.where(me == 0, 2, jnp.where(me == R - 1, 0, 1))
-
-    @pl.when(later > 0)
-    def _():
-        pl.semaphore_wait(hello.at[0], later)
+    if compact:
+        hear(2)
+    else:
+        later = R - 1 - me - jnp.where(me == 0, 2, jnp.where(me == R - 1, 0, 1))
+
+        @pl.when(later > 0)
+        def _():
+            pl.semaphore_wait(hello.at[0], later)
 
     receive_rows(range(1))
     coarse_moment(me, 2)
@@ -404,6 +440,12 @@
         @pl.when(leads & (parity == high))
         def _():
             send_edge(xw, 1, high, cut, leaf)
+
+    for high in (0, 1):
+
+        @pl.when(jnp.logical_not(leads | first_chip) & (parity == high))
+        def _():
+            send_edge(xw, 1, high, 0, TRAIL * leaf // 8)
 
     whole(near_edges, load_sem.at[0]).wait()
     part[0] = near_terms(0, near_edges, 0, 0, 1).astype(BF16)
@@ -432,7 +474,7 @@
 
         @pl.when(jnp.logical_not(leads | first_chip) & (parity == high))
         def _():
-            send_edge(xw, 1, high)
+            send_edge(xw, 1, high, TRAIL * leaf // 8, leaf)
 
     whole(cw0.at[pl.ds(0, 5)], halo_recv.at[0]).wait()
     for level in range(3):
@@ -457,7 +499,7 @@
 
         receive_rows(range(1, 2))
         coarse_moment(near_by, 4 * parity)
-        gather_copy(near_by, twin, 2).start()
+        gather_copy(near_by, twin, 1).start()
 
     for i in range(2):
         row = 2 * R + 2 * me + i
@@ -487,7 +529,7 @@
 
             @pl.when(other < coarse_blocks)
             def _():
-                spot = table_recv.at[other]
+                spot = rows_recv.at[1 + other]
                 send(theirs, theirs, sent.at[3], spot, me, other).wait_recv()
 
     def upper_rows():
@@ -503,9 +545,8 @@
     if compact:
         beyond = ring(-2 * step)
         gather_copy(beyond, me, 0).wait_recv()
-        gather_copy(beyond, twin, 2).start()
-        whole(cr.at[pl.ds(0, 2)], gather_recv.at[1]).wait()
-        whole(cr.at[pl.ds(0, 2)], gather_recv.at[2]).wait()
+        gather_copy(beyond, twin, 1).start()
+        whole(cr.at[pl.ds(0, 4)], gather_recv.at[1]).wait()
         passes = 5
     else:
         for k in range(1, R // 2):
@@ -661,10 +702,9 @@
             dma((6 if R == 8 else 5,)),
             dma((1,)),
             dma((2,)),
-            dma((1 if R == 8 else T,)),
-            dma((3 if R == 8 else R,)),
-            dma((5 if R == 8 else 1,)),
-            pltpu.SemaphoreType.REGULAR((2,)),
+            dma((2 if R == 8 else R,)),
+            dma((5 if R == 8 else 1 + T,)),
+            pltpu.SemaphoreType.REGULAR((4 if R == 8 else 2,)),
         ],
         compiler_params=pltpu.CompilerParams(
             collective_id=0, has_side_effects=True, vmem_limit_bytes=40 * MIB

time: 17.1 us -> 16.8 us (0.982)
  Pallas kernels: 16.9 us -> 16.7 us
    pallas_call x1, Pallas kernels: 14.7 us -> 14.5 us  [body(): pl.pallas_call(lambda *refs: kernel(dims, *refs), name='tree_apply', out_...]
where the time goes in v4:
time: 16.8 us; the launch traced here: 16.7 us
  Pallas kernels  16.7 us (99%)
    pallas_call x1, Pallas kernels, body(): pl.pallas_call(lambda *refs: kernel(dims, *refs), name='tree_apply', out_...  14.5 us
    pallas_call x1, Pallas kernels, body(): pl.pallas_call(finish, name='far_add', out_shape=jax.ShapeDtypeStruct((co...  2.2 us

profile of v4, /device:TPU:1, one launch (start us, length us, event | category | flops | bytes accessed | tf_op | source)
XLA Modules:
  0.0 16.7 jit_solution(7395599282296571538)
XLA Ops:
  0.0 14.5 %tree_apply.1 = (bf16[16,256,512]{2,1,0:T(8,128)(2,1)S(1)}, bf16[16,256,64]{2,1,0:T(8,128)(2,1)S(1)}, bf16[16,32,512]{2,1,0:T(8,128)(2,1)S(1)}, bf16[2,32,512]{2...) custom-call(bf16[16,256,512]{2,1,0:T(8,128)(2,1)} %bitcast.7, ...), custom_call_target="tpu_custom_call" | custom-call | tf_op jit(solution)/shard_map/tree_apply/pallas_call | solution.py:662
  14.5 2.2 %far_add.1 = bf16[16,256,512]{2,1,0:T(8,128)(2,1)} custom-call(bf16[16,256,512]{2,1,0:T(8,128)(2,1)S(1)} %get-tuple-element.11.part, bf16[16,256,64]{2,1,0:T(8,128)(2,1)S(1)} %get-tuple-element.12.tt, bf16[16,32,512]{2,1,0:T(8,128)(2,1)S(1)} %get-tuple-element.13.f, bf16[2,32,512]{2,1,0:T(8,128)(2,1)S(1)} %get-tuple-element.14.top, ...), custom_call_target="tpu_custom_call" | custom-call | tf_op jit(solution)/shard_map/far_add/pallas_call | solution.py:725

commit v5 on v4

--- a/solution.py
+++ b/solution.py
@@ -118,14 +118,12 @@
     load(sc_hbm, coarse_in.at[:, pl.ds(0, 3)], 1)
     load_sb = load(sb_hbm, sb, 2)
     x_loads = [
-        load(x_hbm.at[pl.ds(a, b - a)], xw.at[pl.ds(1 + a, b - a)], 7 + c)
+        load(x_hbm.at[pl.ds(a, b - a)], xw.at[pl.ds(1 + a, b - a)], 5 + c)
         for c, (a, b) in enumerate(spans)
     ]
     load_ef = load(ef_hbm, ef, 3)
     load_lists = [
         load(near_list_hbm, near_list, 4),
-        load(far_fine_hbm, far_fine, 5),
-        load(far_coarse_hbm, far_coarse, 6),
     ]
 
     def send(src, dst, send_sem, recv_sem, row, col):
@@ -275,7 +273,7 @@
             send_rows(urgent, False)
 
     near_loads = [
-        pltpu.make_async_copy(near_hbm.at[pl.ds(a, b - a)], nears[c], load_sem.at[7 + c])
+        pltpu.make_async_copy(near_hbm.at[pl.ds(a, b - a)], nears[c], load_sem.at[5 + c])
         for c, (a, b) in enumerate(spans)
     ]
     edge_loads = [
@@ -413,6 +411,8 @@
 
     send_rows(later_sets, False)
     send_tables(False)
+    far_lists = [load(far_fine_hbm, far_fine, 5), load(far_coarse_hbm, far_coarse, 6)]
+
     if compact:
         hear(2)
     else:
@@ -500,6 +500,9 @@
         receive_rows(range(1, 2))
         coarse_moment(near_by, 4 * parity)
         gather_copy(near_by, twin, 1).start()
+
+    for copy in far_lists:
+        copy.wait()
 
     for i in range(2):
         row = 2 * R + 2 * me + i
@@ -621,8 +624,14 @@
         if t in (0, count - 1):
             matrix = jnp.concatenate([edge_block[t // (count - 1)], matrix], axis=1)
             rows = jnp.concatenate([beyond_leaf[t // (count - 1)], rows], axis=0)
-        out[t] = (part[t].astype(F32) + dot(matrix, rows)).astype(BF16)
-        pltpu.make_async_copy(out.at[t], out_hbm.at[t], sem).start()
+        parts = 4 if t == order[0] else 1
+        size = part.shape[1] // parts
+        for k in range(parts):
+            span = slice(k * size, (k + 1) * size)
+            total = part[t, span].astype(F32) + dot(matrix[span], rows)
+            out[t, span] = total.astype(BF16)
+            spot = pl.ds(k * size, size)
+            pltpu.make_async_copy(out.at[t, spot], out_hbm.at[t, spot], sem).start()
     pltpu.make_async_copy(out, out_hbm, sem).wait()
 
 
@@ -698,7 +707,7 @@
             pltpu.VMEM((4, 2 * rank, 4 * rank), BF16),
             pltpu.VMEM((count // 2, rank, rank), BF16),
             pltpu.VMEM((count, rank, rank), BF16),
-            dma((7 + len(spans),)),
+            dma((5 + len(spans),)),
             dma((6 if R == 8 else 5,)),
             dma((1,)),
             dma((2,)),

time: 16.8 us -> 16.8 us (level)
  no operation moved by 1% of the time
where the time goes in v5:
time: 16.8 us; the launch traced here: 16.6 us
  Pallas kernels  16.6 us (99%)
    pallas_call x1, Pallas kernels, body(): pl.pallas_call(lambda *refs: kernel(dims, *refs), name='tree_apply', out_...  14.4 us
    pallas_call x1, Pallas kernels, body(): pl.pallas_call(finish, name='far_add', out_shape=jax.ShapeDtypeStruct((co...  2.2 us

profile of v5, /device:TPU:1, one launch (start us, length us, event | category | flops | bytes accessed | tf_op | source)
XLA Modules:
  0.0 16.6 jit_solution(10613105669861865047)
XLA Ops:
  0.0 14.4 %tree_apply.1 = (bf16[16,256,512]{2,1,0:T(8,128)(2,1)S(1)}, bf16[16,256,64]{2,1,0:T(8,128)(2,1)S(1)}, bf16[16,32,512]{2,1,0:T(8,128)(2,1)S(1)}, bf16[2,32,512]{2...) custom-call(bf16[16,256,512]{2,1,0:T(8,128)(2,1)} %bitcast.7, ...), custom_call_target="tpu_custom_call" | custom-call | tf_op jit(solution)/shard_map/tree_apply/pallas_call | solution.py:671
  14.4 2.2 %far_add.1 = bf16[16,256,512]{2,1,0:T(8,128)(2,1)} custom-call(bf16[16,256,512]{2,1,0:T(8,128)(2,1)S(1)} %get-tuple-element.11.part, bf16[16,256,64]{2,1,0:T(8,128)(2,1)S(1)} %get-tuple-element.12.tt, bf16[16,32,512]{2,1,0:T(8,128)(2,1)S(1)} %get-tuple-element.13.f, bf16[2,32,512]{2,1,0:T(8,128)(2,1)S(1)} %get-tuple-element.14.top, ...), custom_call_target="tpu_custom_call" | custom-call | tf_op jit(solution)/shard_map/far_add/pallas_call | solution.py:734
